TPU v7x, 32 devices: a whole 2x2x4 slice. The times are simulated.
32 devices in a mesh: freq: 4 (over y, core), lat: 8 (over z, x).
Axes of the slice: x: 2, y: 2, z: 4, core: 2. Of those that a mesh axis runs over, the one named last changes fastest.
Arguments:
- spectra: float32 [2, 4, 32768], P(None, None, ('freq', 'lat')), may hold values from -6 to 6
- tile_route: int32 [32768, 1], P(('freq', 'lat')), may hold values from 0 to 255; in each aligned block of 1024 rows (0 to 1023, 1024 to 2047, ...) at most 8 rows name the same one
- bin_in_tile: int32 [32768], P(('freq', 'lat')), may hold values from 0 to 1023
- trace_offset: float32 [2, 32768], P(None, ('freq', 'lat')), may hold values from -0.5 to 0.5
- weights: float32 [32768], P(('freq', 'lat')), may hold values from 0.2 to 5
- frequency: float32 [4], P('freq'), may hold values from 0.5 to 1.5
- slowness: float32 [2, 8], replicated, may hold values from 0.6 to 1.6
- vel_index: int32 [2, 512, 512], P(None, 'lat'), may hold values from 0 to 7
Outputs:
- wavefield: float32 [2, 4, 512, 512], P(None, 'freq', 'lat')
- depth_image: float32 [2, 512, 512], P(None, 'lat', 'freq')
Inputs may be any that keep to these rules, and one draw needn't show every extreme that they name: `tile_route`: tiles of 32 x 32 bins, numbered row by row over the grid; among the rows of one device no tile is named by more than 8 traces. `bin_in_tile`: row * 32 + column of the bin within the tile.
All inputs are finite; a program needn't handle non-finite values.
Results may differ from a plain program's by a relative error of at most 0.0003.
Values sent between devices are 32-bit elements; how exact they have to be, the bound alone decides.
A program may use at most 64 MiB of HBM per device.

v0:
```python
import functools
import math

import jax
import jax.numpy as jnp
import numpy as np
from jax import lax
from jax.experimental import pallas as pl
from jax.experimental.pallas import tpu as pltpu
from jax.sharding import PartitionSpec as P

TB = 32
MODES = 8
CAP = 8
TERMS = MODES * MODES

damping = 1.0
depth_step = 1.0

NN = (((1,), (0,)), ((), ()))
NT = (((1,), (1,)), ((), ()))
VMEM = pl.BlockSpec(memory_space=pltpu.VMEM)


def dft_tables(length):
    at = np.arange(length)
    angle = 2.0 * math.pi / length * (at[:, None] * at[None, :] % length)
    exact = np.stack([np.cos(angle), np.sin(angle)], 0)
    high = exact.astype(jnp.bfloat16)
    low = (exact - high.astype(np.float64)).astype(jnp.bfloat16)
    return high, low


def mode_tables(length):
    at = np.arange(length)
    angle = 2.0 * math.pi / length * (at[:, None] * at[None, :] % length)
    cosines = np.cos(math.pi * np.arange(MODES)[:, None] * (np.arange(TB)[None, :] + 0.5) / TB)
    fold = np.zeros((length // TB, MODES, length))
    for tile in range(length // TB):
        fold[tile, :, tile * TB : (tile + 1) * TB] = cosines
    fold = fold.reshape(length // TB * MODES, length)
    return np.concatenate([fold @ np.cos(angle), -(fold @ np.sin(angle))], 1).astype(np.float32)


def split2(x):
    high = x.astype(jnp.bfloat16)
    return high, (x - high.astype(jnp.float32)).astype(jnp.bfloat16)


def dot3(a, b, dims=NN):
    one = functools.partial(lax.dot_general, dimension_numbers=dims, preferred_element_type=jnp.float32)
    return one(a[0], b[0]) + (one(a[0], b[1]) + one(a[1], b[0]))


def route_kernel(slot_ref, feat_ref, out_ref):
    feats = feat_ref[...]
    high = feats.astype(jnp.bfloat16)
    rest = feats - high.astype(jnp.float32)
    middle = rest.astype(jnp.bfloat16)
    low = (rest - middle.astype(jnp.float32)).astype(jnp.bfloat16)
    parts = jnp.concatenate([high, middle, low], 0)
    rows = feats.shape[0]
    slot = slot_ref[...]
    width = 256
    for at in range(0, out_ref.shape[1], width):
        places = lax.broadcasted_iota(jnp.int32, (width, slot.shape[1]), 0) + at
        chosen = jnp.where(places == slot, 1.0, 0.0).astype(jnp.bfloat16)
        got = lax.dot_general(parts, chosen, NT, preferred_element_type=jnp.float32)
        out_ref[:, at : at + width] = got[:rows] + got[rows : 2 * rows] + got[2 * rows :]


def fit_kernel(tiles, got_ref, out_ref, system):
    count = got_ref.shape[1]
    data_rows = got_ref.shape[0] - 3
    weight = got_ref[data_rows : data_rows + 1, :]

    def chebyshev(cosine):
        terms = [jnp.ones_like(cosine), cosine]
        for _ in range(MODES - 2):
            terms.append(2.0 * cosine * terms[-1] - terms[-2])
        return terms

    along_x = chebyshev(got_ref[data_rows + 1 : data_rows + 2, :])
    along_y = jnp.concatenate(chebyshev(got_ref[data_rows + 2 : data_rows + 3, :]), 0)
    basis = jnp.concatenate([term * along_y for term in along_x], 0)
    right = jnp.concatenate([basis, got_ref[:data_rows, :]], 0)
    weighted = basis * weight
    lane = lax.broadcasted_iota(jnp.int32, (1, count), 1)
    tile_of = lax.div(lax.rem(lane, tiles * CAP), CAP)
    width = TERMS + data_rows
    eye = jnp.where(
        lax.broadcasted_iota(jnp.int32, (TERMS, width), 0)
        == lax.broadcasted_iota(jnp.int32, (TERMS, width), 1),
        damping,
        0.0,
    )
    left = jnp.concatenate([jnp.where(tile_of == tile, weighted, 0.0) for tile in range(tiles)], 0)
    summed = lax.dot_general(
        left, right, NT, preferred_element_type=jnp.float32, precision=lax.Precision.HIGHEST
    )
    system[...] = summed.reshape(tiles, TERMS, width) + eye[None]
    for k in range(TERMS):
        row = system[:, k : k + 1, :]
        scaled = row * (1.0 / row[:, :, k : k + 1])
        whole = system[...]
        system[...] = whole - whole[:, :, k : k + 1] * scaled
        system[:, k : k + 1, :] = scaled
    out_ref[...] = system[:, :, TERMS:]


def bands(real, imag, out_ref):
    count = out_ref.shape[0]
    band = real.shape[1] // count
    for dst in range(count):
        part = slice(dst * band, (dst + 1) * band)
        out_ref[dst] = jnp.concatenate([real[:, part], imag[:, part]], 1)


def modes_y_kernel(coef_ref, table_ref, out_ref):
    rows = coef_ref.shape[0] // 2
    length = table_ref.shape[1] // 2
    made = lax.dot_general(
        coef_ref[...],
        table_ref[...],
        NN,
        preferred_element_type=jnp.float32,
        precision=lax.Precision.HIGHEST,
    )
    real = made[:rows, :length] - made[rows:, length:]
    imag = made[:rows, length:] + made[rows:, :length]
    bands(real, imag, out_ref)


def swapped(x):
    half = x.shape[1] // 2
    return jnp.concatenate([x[:, half:], x[:, :half]], 1)


def column_kernel(from_modes, high_ref, low_ref, table_ref, got_ref, even_ref, odd_ref, out_ref):
    lanes = got_ref.shape[2]
    got = got_ref[...].reshape(-1, lanes)
    sign = jnp.where(lax.broadcasted_iota(jnp.int32, (1, lanes), 1) < lanes // 2, -1.0, 1.0)
    cosine = (high_ref[0], low_ref[0])
    sine = (high_ref[1], low_ref[1])
    if from_modes:
        length = table_ref.shape[0] // 2
        both = lax.dot_general(
            table_ref[...],
            got,
            NN,
            preferred_element_type=jnp.float32,
            precision=lax.Precision.HIGHEST,
        )
        spectrum = both[:length] + sign * swapped(both[length:])
    else:
        parts = split2(got)
        spectrum = dot3(cosine, parts) - sign * swapped(dot3(sine, parts))
    turned = swapped(spectrum)
    refs = even_ref.shape[0]
    moved = jnp.concatenate(
        [spectrum * even_ref[g] + turned * odd_ref[g] for g in range(refs)], 1
    )
    parts = split2(moved)
    straight = dot3(cosine, parts)
    crossed = dot3(sine, parts)
    rows = out_ref.shape[2]
    for g in range(refs):
        part = slice(g * lanes, (g + 1) * lanes)
        back = straight[:, part] + sign * swapped(crossed[:, part])
        for dst in range(out_ref.shape[0]):
            out_ref[dst, g] = back[dst * rows : (dst + 1) * rows]


def row_kernel(last, high_ref, low_ref, got_ref, cos_ref, sin_ref, group_ref, *out_refs):
    wave_ref = out_refs[0]
    count, refs, rows, lanes = got_ref.shape
    half = lanes // 2
    cosine = (high_ref[0], low_ref[0])
    sine = (high_ref[1], low_ref[1])
    real = jnp.concatenate(
        [got_ref[src, :, :, :half].reshape(refs * rows, half) for src in range(count)], 1
    )
    imag = jnp.concatenate(
        [got_ref[src, :, :, half:].reshape(refs * rows, half) for src in range(count)], 1
    )
    parts = split2(jnp.concatenate([real, imag], 0))
    straight = dot3(parts, cosine)
    crossed = dot3(parts, sine)
    total = refs * rows
    real = straight[:total] - crossed[total:]
    imag = straight[total:] + crossed[:total]
    group = group_ref[...]
    chosen_real, chosen_imag = real[:rows], imag[:rows]
    for g in range(1, refs):
        part = slice(g * rows, (g + 1) * rows)
        chosen_real = jnp.where(group == g, real[part], chosen_real)
        chosen_imag = jnp.where(group == g, imag[part], chosen_imag)
    along, across = cos_ref[...], sin_ref[...]
    real = chosen_real * along - chosen_imag * across
    imag = chosen_real * across + chosen_imag * along
    wave_ref[0] = real
    if last:
        wave_ref[1] = imag
        return
    parts = split2(jnp.concatenate([real, imag], 0))
    straight = dot3(parts, cosine)
    crossed = dot3(parts, sine)
    bands(
        straight[:rows] + crossed[rows:],
        straight[rows:] - crossed[:rows],
        out_refs[1],
    )


def call(kernel, shapes, flops, *operands, scratch=()):
    single = not isinstance(shapes, (list, tuple))
    out_shape = jax.tree.map(
        lambda s: jax.ShapeDtypeStruct(s.shape, jnp.float32), shapes
    )
    return pl.pallas_call(
        kernel,
        out_shape=out_shape,
        in_specs=[VMEM] * len(operands),
        out_specs=VMEM if single else [VMEM] * len(shapes),
        scratch_shapes=list(scratch),
        cost_estimate=pl.CostEstimate(flops=flops, bytes_accessed=4 << 20, transcendentals=0),
        compiler_params=pltpu.CompilerParams(vmem_limit_bytes=48 << 20),
    )(*operands)


def exchange_kernel(count, in_ref, out_ref, sent, landed, kept):
    me = lax.axis_index("lat")
    barrier = pltpu.get_barrier_semaphore()
    partners = [lax.rem(me + step, count) for step in range(1, count)]
    for partner in partners:
        pl.semaphore_signal(
            barrier, inc=1, device_id={"lat": partner}, device_id_type=pl.DeviceIdType.MESH
        )
    pl.semaphore_wait(barrier, count - 1)
    copies = [
        pltpu.make_async_remote_copy(
            src_ref=in_ref.at[partner],
            dst_ref=out_ref.at[me],
            send_sem=sent.at[at],
            recv_sem=landed.at[at],
            device_id={"lat": partner},
            device_id_type=pl.DeviceIdType.MESH,
        )
        for at, partner in enumerate(partners)
    ]
    for copy in copies:
        copy.start()
    own = pltpu.make_async_copy(in_ref.at[me], out_ref.at[me], kept)
    own.start()
    own.wait()
    for copy in copies:
        copy.wait()


def exchange(blocks, number):
    count = blocks.shape[0]
    return pl.pallas_call(
        functools.partial(exchange_kernel, count),
        out_shape=jax.ShapeDtypeStruct(blocks.shape, blocks.dtype),
        in_specs=[pl.BlockSpec(memory_space=pl.ANY)],
        out_specs=pl.BlockSpec(memory_space=pl.ANY),
        scratch_shapes=[
            pltpu.SemaphoreType.DMA((count - 1,)),
            pltpu.SemaphoreType.DMA((count - 1,)),
            pltpu.SemaphoreType.DMA,
        ],
        compiler_params=pltpu.CompilerParams(
            collective_id=number, has_side_effects=True, vmem_limit_bytes=1 << 20
        ),
    )(blocks)


def shaped(*dims):
    return jax.ShapeDtypeStruct(dims, jnp.float32)


def local(spectra, tile_route, bin_in_tile, trace_offset, weights, frequency, slowness, vel_index):
    freq_count = lax.axis_size("freq")
    lat_count = lax.axis_size("lat")
    devices = freq_count * lat_count
    steps, row_count, ny = vel_index.shape
    nx = row_count * lat_count
    total_tiles = (nx // TB) * (ny // TB)
    tiles = total_tiles // devices
    slots = tiles * CAP
    trace_count = spectra.shape[2]
    data_rows = 2 * spectra.shape[1]
    features = data_rows + 3

    tile_id = tile_route[:, 0]
    order = jnp.arange(trace_count)
    rank = jnp.sum(
        ((tile_id[:, None] == tile_id[None, :]) & (order[:, None] < order[None, :])).astype(
            jnp.int32
        ),
        0,
    )
    slab_tiles = total_tiles // lat_count
    owner = (tile_id % slab_tiles) // tiles * lat_count + tile_id // slab_tiles
    slot = owner * slots + (tile_id % tiles) * CAP + rank
    cell_x = (bin_in_tile // TB).astype(jnp.float32) + trace_offset[0]
    cell_y = (bin_in_tile % TB).astype(jnp.float32) + trace_offset[1]
    padded_rows = -(-features // 16) * 16
    feats = jnp.concatenate(
        [
            spectra.reshape(data_rows, trace_count),
            weights[None],
            jnp.cos(math.pi * (cell_x[None] + 0.5) / TB),
            jnp.cos(math.pi * (cell_y[None] + 0.5) / TB),
            jnp.zeros((padded_rows - features, trace_count), jnp.float32),
        ],
        0,
    )
    placed = call(
        route_kernel, shaped(padded_rows, devices * slots), 1 << 28, slot[None], feats
    )
    sent = placed[:features].reshape(features, devices, slots).transpose(1, 0, 2)
    got = lax.all_to_all(sent, ("freq", "lat"), split_axis=0, concat_axis=0, tiled=True)
    got = got.transpose(1, 0, 2).reshape(features, devices * slots)
    coeffs = call(
        functools.partial(fit_kernel, tiles),
        shaped(tiles, TERMS, data_rows),
        1 << 30,
        got,
        scratch=[pltpu.VMEM((tiles, TERMS, TERMS + data_rows), jnp.float32)],
    )
    coeffs = coeffs.reshape(tiles, TERMS, 2, freq_count, -1).transpose(3, 0, 1, 2, 4)
    coeffs = lax.all_to_all(coeffs, "freq", split_axis=0, concat_axis=0, tiled=True)
    tile_rows = row_count // TB
    coeffs = coeffs.reshape(tile_rows, ny // TB, MODES, MODES, 2).transpose(4, 0, 2, 1, 3)
    mode_rows = tile_rows * MODES
    coeffs = coeffs.reshape(2 * mode_rows, ny // TB * MODES)

    high, low = dft_tables(nx)
    table = mode_tables(nx)
    high, low = jnp.asarray(high), jnp.asarray(low)
    table_y, table_x = jnp.asarray(table), jnp.asarray(np.ascontiguousarray(table.T))
    band = ny // lat_count
    refs = 2
    per_group = slowness.shape[1] // refs
    lat_at = lax.axis_index("lat")
    ky_index = lat_at * band + jnp.arange(2 * band) % band
    ky_vals = 2.0 * math.pi / ny * jnp.where(ky_index >= ny // 2, ky_index - ny, ky_index).astype(
        jnp.float32
    )
    kx_index = jnp.arange(nx)
    kx_vals = 2.0 * math.pi / nx * jnp.where(kx_index >= nx // 2, kx_index - nx, kx_index).astype(
        jnp.float32
    )
    odd_sign = jnp.where(jnp.arange(2 * band) < band, -1.0, 1.0)
    inverse_scale = 1.0 / (nx * ny)

    packed = call(
        modes_y_kernel, shaped(lat_count, mode_rows, 2 * band), 1 << 26, coeffs, table_y
    )
    images = []
    for depth_at in range(steps):
        table_row = slowness[depth_at]
        references = table_row.reshape(refs, per_group).mean(axis=1)
        wave_num = frequency[0] * references
        vertical = (
            (wave_num * wave_num)[:, None, None]
            - (kx_vals * kx_vals)[None, :, None]
            - (ky_vals * ky_vals)[None, None, :]
        )
        phase = jnp.sqrt(jnp.maximum(vertical, 0.0)) * depth_step
        damped = jnp.exp(-jnp.sqrt(jnp.maximum(-vertical, 0.0)) * depth_step)
        even = damped * jnp.cos(phase)
        odd = damped * jnp.sin(phase) * odd_sign
        velocity = vel_index[depth_at]
        picked = velocity[None] == jnp.arange(slowness.shape[1])[:, None, None]
        shift_of = (table_row.reshape(refs, per_group) - references[:, None]).reshape(-1)
        split_phase = (
            frequency[0]
            * jnp.sum(jnp.where(picked, shift_of[:, None, None], 0.0), 0)
            * depth_step
        )
        group = velocity // per_group
        along = jnp.cos(split_phase) * inverse_scale
        across = jnp.sin(split_phase) * inverse_scale

        if depth_at == 0:
            columns = lax.all_to_all(packed, "lat", split_axis=0, concat_axis=0, tiled=True)
        else:
            columns = exchange(packed, 2 * depth_at)
        moved = call(
            functools.partial(column_kernel, depth_at == 0),
            shaped(lat_count, refs, row_count, 2 * band),
            1 << 30,
            high,
            low,
            table_x,
            columns,
            even,
            odd,
        )
        rows = exchange(moved, 2 * depth_at + 1)
        last = depth_at == steps - 1
        shapes = [shaped(2 if last else 1, row_count, ny)]
        if not last:
            shapes.append(shaped(lat_count, row_count, 2 * band))
        made = call(
            functools.partial(row_kernel, last),
            shapes,
            1 << 30,
            high,
            low,
            rows,
            along,
            across,
            group,
        )
        wave_field = made[0]
        if not last:
            packed = made[1]
        split = wave_field[0].reshape(row_count, freq_count, ny // freq_count).transpose(1, 0, 2)
        images.append(split)
    split = lax.all_to_all(jnp.stack(images, 1), "freq", split_axis=0, concat_axis=0, tiled=True)
    return (wave_field[:, None], jnp.sum(split, 0))


def solution(mesh):
    return jax.shard_map(
        local,
        mesh=mesh,
        in_specs=(
            P(None, None, ("freq", "lat")),
            P(("freq", "lat"), None),
            P(("freq", "lat")),
            P(None, ("freq", "lat")),
            P(("freq", "lat")),
            P("freq"),
            P(),
            P(None, "lat", None),
        ),
        out_specs=(P(None, "freq", "lat", None), P(None, "lat", "freq")),
        check_vma=False,
    )
```

profile of v0, /device:TPU:0, one launch (start us, length us, event | category | flops | bytes accessed | tf_op | source)
XLA Modules:
  0.0 115.4 jit_solution(5555091469970178287)
XLA Ops:
  2.2 1.2 %convert_reduce_fusion = s32[1024]{0:T(1024)S(1)} fusion(s32[1024]{0:T(1024)} %bitcast.87), kind=kLoop, calls=%fused_computation | loop fusion | flops 5241856 | bytes 8192 | tf_op jit(solution)/shard_map/reduce_sum | solution.py:297
  5.6 1.3 %shard_map.131 = f32[16,2048]{1,0:T(8,128)S(1)} custom-call(s32[1,1024]{1,0:T(1,128)S(1)} %add_add_fusion.slot_ref, f32[16,1024]{1,0:T(8,128)S(1)} %concatenate.3.feat_ref), custom_call_target="tpu_custom_call" | custom-call | flops 268435456 | bytes 4194304 | tf_op jit(solution)/shard_map/pallas_call | solution.py:220
  8.0 7.3 %all-to-all-start = ((f32[32,1,704]{2,1,0:T(1,128)}), f32[32,1,704]{2,1,0:T(1,128)S(1)}, u32[]{:S(2)}, u32[]{:S(2)}) async-start(f32[32,1,704]{2,1,0:T(1,128)} %reshape.374), calls=%async_computation | async-start | bytes 196608 | tf_op jit(solution)/shard_map/all_to_all | solution.py:323
  17.9 5.9 %fusion.17 = (f32[2,512,128]{2,1,0:T(8,128)S(1)}, f32[2,512,128]{2,1,0:T(8,128)}, f32[2,512,128]{2,1,0:T(8,128)}, f32[2,512,128]{2,1,0:T(8,128)}) fusion(f32[2,512]{1,0:T(2,128)S(1)} %get-tuple-element.32, f32[128]{0:T(128)S(1)} %get-tuple-element.44, f32[128]{0:T(128)S(1)} %get-tuple-element.45, f32[2,512]{1,0:T(2,128)S(1)} %get-tuple-element.33), kind=kLoop, calls=%fused_computation.27 | loop fusion | flops 2097152 | bytes 2106368 | tf_op jit(solution)/shard_map/mul | solution.py:374
  25.9 10.4 %shard_map.132 = f32[8,64,8]{2,1,0:T(8,128)S(1)} custom-call(f32[11,2048]{1,0:T(8,128)S(1)} %reshape.358.got_ref), custom_call_target="tpu_custom_call" | custom-call | flops 1073741824 | bytes 4194304 | tf_op jit(solution)/shard_map/pallas_call | solution.py:220
  37.1 3.3 %all-to-all-start.1 = ((f32[4,1,1024]{2,1,0:T(1,128)}), f32[4,1,1024]{2,1,0:T(1,128)S(1)}, u32[]{:S(2)}, u32[]{:S(2)}) async-start(f32[4,1,1024]{2,1,0:T(1,128)} %reshape.376), calls=%async_computation.1 | async-start | bytes 32768 | tf_op jit(solution)/shard_map/all_to_all | solution.py:333
  41.2 3.0 %all-to-all-done.1 = f32[4,1,1024]{2,1,0:T(1,128)S(1)} async-done(((f32[4,1,1024]{2,1,0:T(1,128)}), f32[4,1,1024]{2,1,0:T(1,128)S(1)}, u32[]{:S(2)}, u32[]{:S(2)}) %all-to-all-start.1) | async-done | bytes 16416 | tf_op jit(solution)/shard_map/all_to_all | solution.py:333
  45.8 1.7 %copy.32 = f32[2,2,8,16,8]{4,3,2,1,0:T(8,128)} copy(f32[2,2,8,16,8]{4,2,3,1,0:T(8,128)} %bitcast.76) | data formatting | bytes 32768 | tf_op jit(solution)/shard_map/transpose | solution.py:335
  47.5 1.1 reshape.361.coef_ref
  48.6 1.0 copy-done.4
  49.6 1.1 shard_map.133
  50.7 5.8 %all-to-all-start.2 = ((f32[8,16,128]{2,1,0:T(8,128)}), f32[8,16,128]{2,1,0:T(8,128)S(1)}, u32[]{:S(2)}, u32[]{:S(2)}) async-start(f32[8,16,128]{2,1,0:T(8,128)} %shard_map.133), calls=%async_computation.2 | async-start | bytes 131072 | tf_op jit(solution)/shard_map/all_to_all | solution.py:388
  56.5 2.1 %sine_multiply_fusion = (f32[64,512]{1,0:T(8,128)}, f32[64,512]{1,0:T(8,128)}) fusion(f32[64,512]{1,0:T(8,128)} %select_reduce_fusion, f32[]{:T(128)} %bitcast.71), kind=kLoop, calls=%fused_computation.46 | loop fusion | flops 98304 | bytes 393220 | tf_op jit(solution)/shard_map/mul | solution.py:385
  58.6 4.8 %all-to-all-done.2.got_ref = f32[8,16,128]{2,1,0:T(8,128)S(1)} async-done(((f32[8,16,128]{2,1,0:T(8,128)}), f32[8,16,128]{2,1,0:T(8,128)S(1)}, u32[]{:S(2)}, u32[]{:S(2)}) %all-to-all-start.2) | async-done | bytes 65568 | tf_op jit(solution)/shard_map/all_to_all | solution.py:388
  63.4 1.0 copy-done.5
  64.5 1.0 copy-done.6
  65.5 1.7 %shard_map.134.in_ref = f32[8,2,64,128]{3,2,1,0:T(8,128)S(1)} custom-call(bf16[2,512,512]{2,1,0:T(8,128)(2,1)S(1)} %copy-done, bf16[2,512,512]{2,1,0:T(8,128)(2,1)S(1)} %copy-done.1, f32[1024,128]{1,0:T(8,128)S(1)} %copy-done.2, f32[8,16,128]{2,1,0:T(8,128)S(1)} %all-to-all-done.2.got_ref, f32[2,512,128]{2,1,0:T(8,128)S(1)} %copy-done.5, ...), custom_call_target="tpu_custom_call" | custom-call | flops 1073741824 | bytes 4194304 | tf_op jit(solution)/shard_map/pallas_call | solution.py:220
  67.2 11.1 %shard_map.135.got_ref = f32[8,2,64,128]{3,2,1,0:T(8,128)S(1)} custom-call(f32[8,2,64,128]{3,2,1,0:T(8,128)S(1)} %shard_map.134.in_ref), custom_call_target="tpu_custom_call" | custom-call | tf_op jit(solution)/shard_map/pallas_call | solution.py:262
  78.3 1.7 %shard_map.136 = (f32[1,64,512]{2,1,0:T(8,128)S(1)}, f32[8,64,128]{2,1,0:T(8,128)S(1)}) custom-call(bf16[2,512,512]{2,1,0:T(8,128)(2,1)S(1)} %copy-done, bf16[2,512,512]{2,1,0:T(8,128)(2,1)S(1)} %copy-done.1, f32[8,2,64,128]{3,2,1,0:T(8,128)S(1)} %shard_map.135.got_ref, f32[64,512]{1,0:T(8,128)S(1)} %get-tuple-element.23.cos_ref, ...), custom_call_target="tpu_custom_call" | custom-call | flops 1073741824 | bytes 4194304 | tf_op jit(solution)/shard_map/pallas_call | solution.py:220
  80.1 8.6 %shard_map.137.got_ref = f32[8,64,128]{2,1,0:T(8,128)S(1)} custom-call(f32[8,64,128]{2,1,0:T(8,128)S(1)} %get-tuple-element.4.in_ref), custom_call_target="tpu_custom_call" | custom-call | tf_op jit(solution)/shard_map/pallas_call | solution.py:262
  88.7 2.1 %shard_map.138.in_ref = f32[8,2,64,128]{3,2,1,0:T(8,128)S(1)} custom-call(bf16[2,512,512]{2,1,0:T(8,128)(2,1)S(1)} %copy-done, bf16[2,512,512]{2,1,0:T(8,128)(2,1)S(1)} %copy-done.1, f32[1024,128]{1,0:T(8,128)S(1)} %copy-done.2, f32[8,64,128]{2,1,0:T(8,128)S(1)} %shard_map.137.got_ref, f32[2,512,128]{2,1,0:T(8,128)S(1)} %copy-done.3, ...), custom_call_target="tpu_custom_call" | custom-call | flops 1073741824 | bytes 4194304 | tf_op jit(solution)/shard_map/pallas_call | solution.py:220
  90.8 12.6 %shard_map.139.got_ref = f32[8,2,64,128]{3,2,1,0:T(8,128)S(1)} custom-call(f32[8,2,64,128]{3,2,1,0:T(8,128)S(1)} %shard_map.138.in_ref), custom_call_target="tpu_custom_call" | custom-call | tf_op jit(solution)/shard_map/pallas_call | solution.py:262
  103.5 1.8 %shard_map.140 = f32[2,64,512]{2,1,0:T(8,128)} custom-call(bf16[2,512,512]{2,1,0:T(8,128)(2,1)S(1)} %copy-done, bf16[2,512,512]{2,1,0:T(8,128)(2,1)S(1)} %copy-done.1, f32[8,2,64,128]{3,2,1,0:T(8,128)S(1)} %shard_map.139.got_ref, f32[64,512]{1,0:T(8,128)S(1)} %copy-done.8, f32[64,512]{1,0:T(8,128)S(1)} %copy-done.7, s32[64,512]{1,0:T(8,128)S(1)} %copy-done.11), custom_call_target="tpu_custom_call" | custom-call | flops 1073741824 | bytes 4194304 | tf_op jit(solution)/shard_map/pallas_call | solution.py:220
  106.4 8.4 %all_to_all.20 = f32[4,2,64,128]{3,2,1,0:T(8,128)S(1)} all-to-all(f32[4,2,64,128]{3,2,1,0:T(8,128)S(1)} %pad_maximum_fusion), channel_id=1, replica_groups=mesh['freq'=4,'lat'=8] {'freq'}, dimensions={0} | all-to-all | bytes 524288 | tf_op jit(solution)/shard_map/all_to_all | solution.py:423
  (75 shorter events, 13.8 us)
Async XLA Ops:
  5.6 9.7 %copy-start.13 = (s32[2,64,512]{2,1,0:T(8,128)S(1)}, s32[2,64,512]{2,1,0:T(8,128)}, u32[]{:S(2)}) copy-start(s32[2,64,512]{2,1,0:T(8,128)} %param.19) | copy-start | bytes 786436
  7.0 9.8 %copy-start.14 = (f32[2,8]{1,0:T(2,128)S(1)}, f32[2,8]{1,0:T(2,128)}, u32[]{:S(2)}) copy-start(f32[2,8]{1,0:T(2,128)} %param.18) | copy-start | bytes 196
  8.0 16.3 %all-to-all-start = ((f32[32,1,704]{2,1,0:T(1,128)}), f32[32,1,704]{2,1,0:T(1,128)S(1)}, u32[]{:S(2)}, u32[]{:S(2)}) async-start(f32[32,1,704]{2,1,0:T(1,128)} %reshape.374), calls=%async_computation | async-start | bytes 196608 | tf_op jit(solution)/shard_map/all_to_all | solution.py:323
  37.1 7.1 %all-to-all-start.1 = ((f32[4,1,1024]{2,1,0:T(1,128)}), f32[4,1,1024]{2,1,0:T(1,128)S(1)}, u32[]{:S(2)}, u32[]{:S(2)}) async-start(f32[4,1,1024]{2,1,0:T(1,128)} %reshape.376), calls=%async_computation.1 | async-start | bytes 32768 | tf_op jit(solution)/shard_map/all_to_all | solution.py:333
  40.4 23.1 %copy-start.2 = (f32[1024,128]{1,0:T(8,128)S(1)}, f32[1024,128]{1,0:T(8,128)}, u32[]{:S(2)}) copy-start(f32[1024,128]{1,0:T(8,128)} %constant.147.clone.table_ref) | copy-start | bytes 1572868
  45.0 18.5 %copy-start = (bf16[2,512,512]{2,1,0:T(8,128)(2,1)S(1)}, bf16[2,512,512]{2,1,0:T(8,128)(2,1)}, u32[]{:S(2)}) copy-start(bf16[2,512,512]{2,1,0:T(8,128)(2,1)} %constant.144.clone.high_ref) | copy-start | bytes 3145732
  45.0 18.5 %copy-start.1 = (bf16[2,512,512]{2,1,0:T(8,128)(2,1)S(1)}, bf16[2,512,512]{2,1,0:T(8,128)(2,1)}, u32[]{:S(2)}) copy-start(bf16[2,512,512]{2,1,0:T(8,128)(2,1)} %constant.145.clone.low_ref) | copy-start | bytes 3145732
  48.6 1.0 copy-start.4
  50.7 12.7 %all-to-all-start.2 = ((f32[8,16,128]{2,1,0:T(8,128)}), f32[8,16,128]{2,1,0:T(8,128)S(1)}, u32[]{:S(2)}, u32[]{:S(2)}) async-start(f32[8,16,128]{2,1,0:T(8,128)} %shard_map.133), calls=%async_computation.2 | async-start | bytes 131072 | tf_op jit(solution)/shard_map/all_to_all | solution.py:388
  63.4 1.0 copy-start.5
  64.5 1.0 copy-start.6
  67.2 11.1 %copy-start.12 = (s32[64,512]{1,0:T(8,128)S(1)}, s32[64,512]{1,0:T(8,128)}, u32[]{:S(2)}) copy-start(s32[64,512]{1,0:T(8,128)} %get-tuple-element.17.group_ref) | copy-start | bytes 393220
  78.3 10.4 %copy-start.3 = (f32[2,512,128]{2,1,0:T(8,128)S(1)}, f32[2,512,128]{2,1,0:T(8,128)}, u32[]{:S(2)}) copy-start(f32[2,512,128]{2,1,0:T(8,128)} %get-tuple-element.27.even_ref) | copy-start | bytes 1572868
  80.1 8.7 %copy-start.9 = (f32[1,64,512]{2,1,0:T(8,128)}, f32[1,64,512]{2,1,0:T(8,128)S(1)}, u32[]{:S(2)}) copy-start(f32[1,64,512]{2,1,0:T(8,128)S(1)} %get-tuple-element.5) | copy-start | bytes 393220
  90.8 12.6 %copy-start.7 = (f32[64,512]{1,0:T(8,128)S(1)}, f32[64,512]{1,0:T(8,128)}, u32[]{:S(2)}) copy-start(f32[64,512]{1,0:T(8,128)} %get-tuple-element.20.sin_ref) | copy-start | bytes 393220
  90.8 12.6 %copy-start.8 = (f32[64,512]{1,0:T(8,128)S(1)}, f32[64,512]{1,0:T(8,128)}, u32[]{:S(2)}) copy-start(f32[64,512]{1,0:T(8,128)} %get-tuple-element.21.cos_ref) | copy-start | bytes 393220
  90.8 12.6 %copy-start.11 = (s32[64,512]{1,0:T(8,128)S(1)}, s32[64,512]{1,0:T(8,128)}, u32[]{:S(2)}) copy-start(s32[64,512]{1,0:T(8,128)} %get-tuple-element.16.group_ref) | copy-start | bytes 393220
  103.5 2.8 %copy-start.10 = (f32[1,64,512]{2,1,0:T(8,128)S(1)}, f32[1,64,512]{2,1,0:T(8,128)}, u32[]{:S(2)}) copy-start(f32[1,64,512]{2,1,0:T(8,128)} %copy-done.9) | copy-start | bytes 393220
where the time goes:
time: 117 us; the launch traced here: 115 us
  Pallas kernels  52.3 us (45%)
  starting transfers between devices  16.4 us (14%)
  other arithmetic  15.5 us (13%)
  local copies, waits for them, and re-layouts  13.3 us (11%)
  blocking collectives  8.39 us (7%)
  waiting for transfers between devices  7.81 us (7%)
  between operations  1.66 us (1%)
    pallas_call x3, Pallas kernels, exchange(): pl.pallas_call(functools.partial(exchange_kernel, count), out_shape=jax.S...  32.3 us
    pallas_call x7, Pallas kernels, call(): pl.pallas_call(kernel, out_shape=out_shape, in_specs=[VMEM] * len(operand...  20 us
    all_to_all x1, blocking collectives, local(): lax.all_to_all(jnp.stack(images, 1), 'freq', split_axis=0, concat_axis=0,...  8.39 us
    all_to_all x1, starting transfers between devices, local(): lax.all_to_all(sent, ('freq', 'lat'), split_axis=0, concat_axis=0, tiled=...  7.33 us
    mul x1, other arithmetic, local(): odd = damped * jnp.sin(phase) * odd_sign  5.86 us
    all_to_all x1, starting transfers between devices, local(): lax.all_to_all(packed, 'lat', split_axis=0, concat_axis=0, tiled=True)  5.81 us
    unnamed x34, local copies, waits for them, and re-layouts  4.84 us
    all_to_all x1, waiting for transfers between devices, local(): lax.all_to_all(packed, 'lat', split_axis=0, concat_axis=0, tiled=True)  4.82 us
  transfers between devices with their start and end apart: 3, of which 2 were waited for; matrix products, arithmetic and copies ran while one was open for 10% of the time, Pallas kernels for 0%

commit v1 on v0

v1 whole, which is shorter than its diff:
```python
import functools
import math

import jax
import jax.numpy as jnp
import numpy as np
from jax import lax
from jax.experimental import pallas as pl
from jax.experimental.pallas import tpu as pltpu
from jax.sharding import PartitionSpec as P

TB = 32
MODES = 8
CAP = 8
TERMS = MODES * MODES
REFS = 2

damping = 1.0
depth_step = 1.0

NN = (((1,), (0,)), ((), ()))
NT = (((1,), (1,)), ((), ()))
VMEM = pl.BlockSpec(memory_space=pltpu.VMEM)
SMEM = pl.BlockSpec(memory_space=pltpu.SMEM)
ANY = pl.BlockSpec(memory_space=pl.ANY)
MESH = pl.DeviceIdType.MESH


def two_parts(exact):
    high = exact.astype(jnp.bfloat16)
    low = (exact - high.astype(np.float64)).astype(jnp.bfloat16)
    return np.stack([high, low], 0)


def hartley(length):
    at = np.arange(length)
    angle = 2.0 * math.pi / length * (at[:, None] * at[None, :] % length)
    return (np.cos(angle) + np.sin(angle)) / math.sqrt(length)


def mode_table(length):
    cosines = np.cos(math.pi * np.arange(MODES)[:, None] * (np.arange(TB)[None, :] + 0.5) / TB)
    fold = np.zeros((length // TB, MODES, length))
    for tile in range(length // TB):
        fold[tile, :, tile * TB : (tile + 1) * TB] = cosines
    return fold.reshape(length // TB * MODES, length) @ hartley(length)


def split2(x):
    high = x.astype(jnp.bfloat16)
    return high, (x - high.astype(jnp.float32)).astype(jnp.bfloat16)


def dot(a, b, dims=NN):
    return lax.dot_general(a, b, dims, preferred_element_type=jnp.float32)


def dot3(a, b, dims=NN):
    return dot(a[0], b[0], dims) + (dot(a[0], b[1], dims) + dot(a[1], b[0], dims))


def series(value, first, count):
    total = jnp.full(value.shape, 1.0 / math.factorial(2 * (count - 1) + first), jnp.float32)
    for n in range(count - 2, -1, -1):
        total = 1.0 / math.factorial(2 * n + first) - value * total
    return total


def cosine_of(cell):
    angle = (0.5 * TB - (cell + 0.5)) * (math.pi / TB)
    return angle * series(angle * angle, 1, 9)


def propagator(wave_squared, kx, ky):
    vertical = wave_squared - kx * kx - ky * ky
    root = jnp.sqrt(jnp.abs(vertical)) * depth_step
    squared = root * root
    moving = vertical > 0.0
    even = jnp.where(moving, series(squared, 0, 10), jnp.exp(-root))
    odd = jnp.where(moving, root * series(squared, 1, 10), 0.0)
    return even, odd


def signed(index, length):
    return (
        2.0 * math.pi / length * jnp.where(index >= length // 2, index - length, index).astype(jnp.float32)
    )


def iota(shape, axis):
    return lax.broadcasted_iota(jnp.int32, shape, axis)


def program(
    cfg,
    spectra_ref,
    tile_ref,
    bin_ref,
    offset_ref,
    weight_ref,
    freq_ref,
    slow_ref,
    vel_hbm,
    hart_hbm,
    modes_hbm,
    modes_t_hbm,
    wave_ref,
    image_ref,
    hart,
    modes,
    modes_t,
    vel,
    route_out,
    route_in,
    system,
    coef_out,
    coef_in,
    wide_even,
    wide_odd,
    band_even,
    band_odd,
    along,
    across,
    fwd_out,
    fwd_in,
    back_out,
    back_in,
    image_out,
    image_in,
    table_sem,
    route_sent,
    route_got,
    coef_sent,
    coef_got,
    fwd_sent,
    fwd_got,
    back_sent,
    back_got,
    image_sent,
    image_got,
):
    F, L, tiles, nx, ny, rows, band, data_rows, padded, steps, nvel = cfg
    devices = F * L
    slots = tiles * CAP
    per_group = nvel // REFS
    lanes = 2 * band
    me_f = lax.axis_index("freq")
    me_l = lax.axis_index("lat")
    me = me_l * F + me_f

    loads = [
        pltpu.make_async_copy(src, dst, table_sem.at[at])
        for at, (src, dst) in enumerate(
            [(vel_hbm, vel), (modes_hbm, modes), (modes_t_hbm, modes_t), (hart_hbm, hart)]
        )
    ]
    for load in loads:
        load.start()

    barrier = pltpu.get_barrier_semaphore()

    def partner_of(step):
        other = lax.rem(me + step, devices)
        return other, {"freq": lax.rem(other, F), "lat": lax.div(other, F)}

    def greet(step, carry):
        _, device = partner_of(step)
        pl.semaphore_signal(barrier, inc=1, device_id=device, device_id_type=MESH)
        return carry

    lax.fori_loop(1, devices, greet, 0)

    count = tile_ref.shape[1]
    width = 128
    tile = tile_ref[...]
    columns = [
        jnp.transpose(jnp.broadcast_to(tile[:, at : at + width], (width, width)))
        for at in range(0, count, width)
    ]
    earlier = iota((width, width), 0) < iota((width, width), 1)
    ranks = []
    for at in range(count // width):
        row = jnp.broadcast_to(tile[:, at * width : (at + 1) * width], (width, width))
        same = jnp.where((columns[at] == row) & earlier, 1, 0)
        for before in range(at):
            same = same + jnp.where(columns[before] == row, 1, 0)
        ranks.append(jnp.sum(same, 0, keepdims=True))
    rank = jnp.concatenate(ranks, 1)
    turned = lax.rem(lax.rem(tile, tiles) + me, tiles)
    slot = lax.div(tile, tiles) * slots + turned * CAP + rank

    cell = bin_ref[...]
    root_weight = jnp.sqrt(weight_ref[...])
    cell_x = lax.div(cell, TB).astype(jnp.float32) + offset_ref[0:1, :]
    cell_y = lax.rem(cell, TB).astype(jnp.float32) + offset_ref[1:2, :]
    feats = jnp.concatenate(
        [spectra_ref[0] * root_weight, spectra_ref[1] * root_weight]
        + [root_weight, cosine_of(cell_x), cosine_of(cell_y)]
        + [jnp.zeros((padded - data_rows - 3, count), jnp.float32)],
        0,
    )
    high = feats.astype(jnp.bfloat16)
    rest = feats - high.astype(jnp.float32)
    middle = rest.astype(jnp.bfloat16)
    low = (rest - middle.astype(jnp.float32)).astype(jnp.bfloat16)
    parts = jnp.concatenate([high, middle, low], 0)
    wide = 256
    for at in range(0, devices * slots, wide):
        places = iota((wide, count), 0) + at
        chosen = jnp.where(places == slot, 1.0, 0.0).astype(jnp.bfloat16)
        got = dot(parts, chosen, NT)
        got = got[:padded] + got[padded : 2 * padded] + got[2 * padded :]
        for piece in range(wide // slots):
            route_out[at // slots + piece] = got[:, piece * slots : (piece + 1) * slots]

    pl.semaphore_wait(barrier, devices - 1)

    def spread(out, into, sent, landed):
        def copy_of(step):
            other, device = partner_of(step)
            return pltpu.make_async_remote_copy(
                src_ref=out.at[other] if out.shape[0] == devices else out.at[lax.rem(other, F)],
                dst_ref=into.at[me],
                send_sem=sent.at[step],
                recv_sem=landed.at[step],
                device_id=device,
                device_id_type=MESH,
            )

        def start(step, carry):
            copy_of(step).start()
            return carry

        def arrive(step, carry):
            copy_of(step).wait_recv()
            return carry

        def leave(step, carry):
            copy_of(step).wait_send()
            return carry

        lax.fori_loop(1, devices, start, 0)
        return (
            lambda: lax.fori_loop(1, devices, arrive, 0),
            lambda: lax.fori_loop(1, devices, leave, 0),
        )

    arrive, leave_route = spread(route_out, route_in, route_sent, route_got)
    route_in[pl.ds(me, 1)] = route_out[pl.ds(me, 1)]

    frequency = freq_ref[0]
    waves = []
    for depth_at in range(steps):
        squares = []
        for g in range(REFS):
            total = slow_ref[depth_at, g * per_group]
            for i in range(1, per_group):
                total = total + slow_ref[depth_at, g * per_group + i]
            reference = total * (1.0 / per_group)
            squares.append((reference, (frequency * reference) * (frequency * reference)))
        waves.append(squares)

    chunk = 8

    def wide_tables(at, carry):
        first = pl.multiple_of(at * chunk, chunk)
        kx = signed(iota((chunk, ny), 0) + first, nx)
        ky = signed(iota((chunk, ny), 1), ny)
        for g in range(REFS):
            even, odd = propagator(waves[0][g][1], kx, ky)
            wide_even[g, pl.ds(first, chunk), :] = even
            wide_odd[g, pl.ds(first, chunk), :] = odd
        return carry

    lax.fori_loop(0, nx // chunk, wide_tables, 0)
    arrive()

    group_at = lax.div(iota((padded, slots), 1), CAP)
    eye = jnp.where(iota((TERMS, TERMS + data_rows), 0) == iota((TERMS, TERMS + data_rows), 1), damping, 0.0)

    def chebyshev(cosine):
        terms = [jnp.ones_like(cosine), cosine]
        for _ in range(MODES - 2):
            terms.append(2.0 * cosine * terms[-1] - terms[-2])
        return terms

    for t in range(tiles):
        pieces = []
        for first in range(0, devices, tiles):
            picked = route_in[first]
            for i in range(1, tiles):
                picked = jnp.where(group_at == (t + i) % tiles, route_in[first + i], picked)
            pieces.append(picked)
        got = jnp.concatenate(pieces, 1)
        scale = got[data_rows : data_rows + 1]
        along_x = chebyshev(got[data_rows + 1 : data_rows + 2])
        along_y = jnp.concatenate(chebyshev(got[data_rows + 2 : data_rows + 3]), 0)
        basis = jnp.concatenate([(term * scale) * along_y for term in along_x], 0)
        right = jnp.concatenate([basis, got[:data_rows]], 0)
        system[t] = eye + lax.dot_general(
            basis, right, NT, preferred_element_type=jnp.float32, precision=lax.Precision.HIGHEST
        )
    for k in range(TERMS):
        row = system[:, k : k + 1, :]
        scaled = row * (1.0 / row[:, :, k : k + 1])
        whole = system[...]
        system[...] = whole - whole[:, :, k : k + 1] * scaled
        system[:, k : k + 1, :] = scaled
    solved = [jnp.transpose(system[t])[TERMS:] for t in range(tiles)]
    for a in range(MODES):
        line = jnp.concatenate([one[:, a * MODES : (a + 1) * MODES] for one in solved], 1)
        for part in range(2):
            for f in range(F):
                at = part * F + f
                coef_out[f, part, a : a + 1, :] = line[at : at + 1]

    arrive, leave_coef = spread(coef_out, coef_in, coef_sent, coef_got)
    coef_in[pl.ds(me, 1)] = coef_out[pl.ds(me_f, 1)]

    line = iota((chunk, lanes), 1)
    ky = signed(me_l * band + lax.rem(line, band), ny)
    sign = jnp.where(line < band, -1.0, 1.0)

    def band_tables(at, carry):
        first = pl.multiple_of(at * chunk, chunk)
        kx = signed(iota((chunk, lanes), 0) + first, nx)
        for depth_at in range(1, steps):
            for g in range(REFS):
                even, odd = propagator(waves[depth_at][g][1], kx, ky)
                band_even[depth_at - 1, g, pl.ds(first, chunk), :] = even
                band_odd[depth_at - 1, g, pl.ds(first, chunk), :] = odd * sign
        return carry

    lax.fori_loop(0, nx // chunk, band_tables, 0)
    for load in loads:
        load.wait()
    for depth_at in range(steps):
        velocity = vel[depth_at]
        cosine = jnp.zeros(velocity.shape, jnp.float32)
        sine = jnp.zeros(velocity.shape, jnp.float32)
        for i in range(nvel):
            shift = slow_ref[depth_at, i] - waves[depth_at][i // per_group][0]
            angle = jnp.full((8, 128), frequency * shift * depth_step, jnp.float32)
            squared = angle * angle
            cosine_i = series(squared, 0, 9)[0:1, 0:1]
            sine_i = (angle * series(squared, 1, 9))[0:1, 0:1]
            cosine = jnp.where(velocity == i, cosine_i, cosine)
            sine = jnp.where(velocity == i, sine_i, sine)
        along[depth_at] = cosine
        across[depth_at] = sine
    arrive()

    per_row = (ny // TB) // tiles
    lines = []
    for part in range(2):
        for tile_row in range(nx // TB):
            lines.append(
                jnp.concatenate([coef_in[tile_row * per_row + j, part] for j in range(per_row)], 1)
            )
    spread_y = dot3(split2(jnp.concatenate(lines, 0)), (modes[0], modes[1]))
    mode_rows = nx // TB * MODES
    spread_y = split2(jnp.concatenate([spread_y[:mode_rows], spread_y[mode_rows:]], 1))
    own = pl.ds(pl.multiple_of(me_l * rows, rows), rows)
    own_high, own_low = hart[0, own, :], hart[1, own, :]
    both = jnp.concatenate([own_high, own_low], 0)
    half = nx // 2
    backs = [None] * REFS
    for first in range(0, nx, half):
        part = slice(first, first + half)
        spectrum = dot3((modes_t[0, part, :], modes_t[1, part, :]), spread_y)
        real, imag = spectrum[:, :ny], spectrum[:, ny:]
        for g in range(REFS):
            even, odd = wide_even[g, part, :], wide_odd[g, part, :]
            moved = split2(jnp.concatenate([real * even - imag * odd, real * odd + imag * even], 1))
            made = dot(both[:, part], moved[0])
            made = made[:rows] + (made[rows:] + dot(own_high[:, part], moved[1]))
            backs[g] = made if backs[g] is None else backs[g] + made
    lines = [back[:, p * ny : (p + 1) * ny] for back in backs for p in range(2)]

    def to_field(depth_at, lines):
        made = dot3(split2(jnp.concatenate(lines, 0)), (hart[0], hart[1]))
        velocity = vel[depth_at]
        real, imag = made[:rows], made[rows : 2 * rows]
        for g in range(1, REFS):
            chosen = velocity >= g * per_group
            real = jnp.where(chosen, made[2 * g * rows : (2 * g + 1) * rows], real)
            imag = jnp.where(chosen, made[(2 * g + 1) * rows : (2 * g + 2) * rows], imag)
        cosine, sine = along[depth_at], across[depth_at]
        return real * cosine - imag * sine, real * sine + imag * cosine

    def swap(x):
        return jnp.concatenate([x[:, band:], x[:, :band]], 1)

    def send_image(depth_at, real):
        piece = ny // F
        for f in range(F):
            image_out[depth_at, f] = real[:, f * piece : (f + 1) * piece]
        copies = []
        for step in range(1, F):
            other = lax.rem(me_f + step, F)
            copies.append(
                pltpu.make_async_remote_copy(
                    src_ref=image_out.at[depth_at, other],
                    dst_ref=image_in.at[depth_at, me_f],
                    send_sem=image_sent.at[depth_at, step],
                    recv_sem=image_got.at[depth_at, step],
                    device_id={"freq": other},
                    device_id_type=MESH,
                )
            )
        for copy in copies:
            copy.start()
        image_in[depth_at, pl.ds(me_f, 1)] = image_out[depth_at, pl.ds(me_f, 1)]
        return copies

    def exchange(at, out, into, sent, landed):
        copies = []
        for step in range(1, L):
            other = lax.rem(me_l + step, L)
            copies.append(
                pltpu.make_async_remote_copy(
                    src_ref=out.at[at, other],
                    dst_ref=into.at[at, me_l],
                    send_sem=sent.at[at, step],
                    recv_sem=landed.at[at, step],
                    device_id={"lat": other},
                    device_id_type=MESH,
                )
            )
        for copy in copies:
            copy.start()
        into[at, pl.ds(me_l, 1)] = out[at, pl.ds(me_l, 1)]
        return copies

    pending = []
    images = []
    for depth_at in range(steps):
        real, imag = to_field(depth_at, lines)
        images.append(send_image(depth_at, real))
        if depth_at == steps - 1:
            wave_ref[0] = real
            wave_ref[1] = imag
            break
        made = dot3(split2(jnp.concatenate([real, imag], 0)), (hart[0], hart[1]))
        for dst in range(L):
            part = slice(dst * band, (dst + 1) * band)
            fwd_out[depth_at, dst] = jnp.concatenate([made[:rows, part], made[rows:, part]], 1)
        copies = exchange(depth_at, fwd_out, fwd_in, fwd_sent, fwd_got)
        pending += copies
        for copy in copies:
            copy.wait_recv()
        got = split2(fwd_in[depth_at].reshape(nx, lanes))
        made = dot(hart[0], jnp.concatenate([got[0], got[1]], 1))
        spectrum = made[:, :lanes] + (made[:, lanes:] + dot(hart[1], got[0]))
        swapped = swap(spectrum)
        moved = jnp.concatenate(
            [
                spectrum * band_even[depth_at, g] + swapped * band_odd[depth_at, g]
                for g in range(REFS)
            ],
            1,
        )
        back = dot3((hart[0], hart[1]), split2(moved))
        back_out[depth_at] = back.reshape(L, rows, REFS * lanes)
        copies = exchange(depth_at, back_out, back_in, back_sent, back_got)
        pending += copies
        for copy in copies:
            copy.wait_recv()
        lines = [
            jnp.concatenate(
                [back_in[depth_at, src, :, q * band : (q + 1) * band] for src in range(L)], 1
            )
            for q in range(2 * REFS)
        ]

    leave_route()
    leave_coef()
    for copy in pending:
        copy.wait_send()
    for depth_at in range(steps):
        for copy in images[depth_at]:
            copy.wait()
        total = image_in[depth_at, 0]
        for f in range(1, F):
            total = total + image_in[depth_at, f]
        image_ref[depth_at] = total


def local(spectra, tile_route, bin_in_tile, trace_offset, weights, frequency, slowness, vel_index):
    F = lax.axis_size("freq")
    L = lax.axis_size("lat")
    devices = F * L
    steps, rows, ny = vel_index.shape
    nx = rows * L
    tiles = (nx // TB) * (ny // TB) // devices
    slots = tiles * CAP
    count = spectra.shape[2]
    data_rows = 2 * spectra.shape[1]
    padded = -(-(data_rows + 3) // 16) * 16
    band = ny // L
    lanes = 2 * band
    nvel = slowness.shape[1]
    mode_rows = nx // TB * MODES
    cfg = (F, L, tiles, nx, ny, rows, band, data_rows, padded, steps, nvel)

    hart = jnp.asarray(two_parts(hartley(nx)))
    modes = two_parts(mode_table(nx))
    modes_t = jnp.asarray(np.ascontiguousarray(modes.transpose(0, 2, 1)))
    modes = jnp.asarray(modes)

    f32, bf16 = jnp.float32, jnp.bfloat16
    between = max(steps - 1, 1)
    dma = pltpu.SemaphoreType.DMA
    wave, image = pl.pallas_call(
        functools.partial(program, cfg),
        out_shape=[
            jax.ShapeDtypeStruct((2, rows, ny), f32),
            jax.ShapeDtypeStruct((steps, rows, ny // F), f32),
        ],
        in_specs=[VMEM, VMEM, VMEM, VMEM, VMEM, SMEM, SMEM, ANY, ANY, ANY, ANY],
        out_specs=[VMEM, VMEM],
        scratch_shapes=[
            pltpu.VMEM((2, nx, nx), bf16),
            pltpu.VMEM((2, mode_rows, nx), bf16),
            pltpu.VMEM((2, nx, mode_rows), bf16),
            pltpu.VMEM((steps, rows, ny), jnp.int32),
            pltpu.VMEM((devices, padded, slots), f32),
            pltpu.VMEM((devices, padded, slots), f32),
            pltpu.VMEM((tiles, TERMS, TERMS + data_rows), f32),
            pltpu.VMEM((F, 2, MODES, tiles * MODES), f32),
            pltpu.VMEM((devices, 2, MODES, tiles * MODES), f32),
            pltpu.VMEM((REFS, nx, ny), f32),
            pltpu.VMEM((REFS, nx, ny), f32),
            pltpu.VMEM((between, REFS, nx, lanes), f32),
            pltpu.VMEM((between, REFS, nx, lanes), f32),
            pltpu.VMEM((steps, rows, ny), f32),
            pltpu.VMEM((steps, rows, ny), f32),
            pltpu.VMEM((between, L, rows, lanes), f32),
            pltpu.VMEM((between, L, rows, lanes), f32),
            pltpu.VMEM((between, L, rows, REFS * lanes), f32),
            pltpu.VMEM((between, L, rows, REFS * lanes), f32),
            pltpu.VMEM((steps, F, rows, ny // F), f32),
            pltpu.VMEM((steps, F, rows, ny // F), f32),
            dma((4,)),
            dma((devices,)),
            dma((devices,)),
            dma((devices,)),
            dma((devices,)),
            dma((between, L)),
            dma((between, L)),
            dma((between, L)),
            dma((between, L)),
            dma((steps, F)),
            dma((steps, F)),
        ],
        compiler_params=pltpu.CompilerParams(
            collective_id=0, has_side_effects=True, vmem_limit_bytes=56 << 20
        ),
    )(
        spectra,
        tile_route.reshape(1, count),
        bin_in_tile.reshape(1, count),
        trace_offset,
        weights.reshape(1, count),
        frequency,
        slowness,
        vel_index,
        hart,
        modes,
        modes_t,
    )
    return wave[:, None], image


def solution(mesh):
    return jax.shard_map(
        local,
        mesh=mesh,
        in_specs=(
            P(None, None, ("freq", "lat")),
            P(("freq", "lat"), None),
            P(("freq", "lat")),
            P(None, ("freq", "lat")),
            P(("freq", "lat")),
            P("freq"),
            P(),
            P(None, "lat", None),
        ),
        out_specs=(P(None, "freq", "lat", None), P(None, "lat", "freq")),
        check_vma=False,
    )
```

time: 117 us -> 63.6 us (0.54)
  starting transfers between devices: 16.4 us -> 0 us
  other arithmetic: 15.5 us -> 0 us
  local copies, waits for them, and re-layouts: 13.3 us -> 2.34 us
  blocking collectives: 8.39 us -> 0 us
  waiting for transfers between devices: 7.81 us -> 0 us
  Pallas kernels: 52.3 us -> 59.1 us
    all_to_all x3 -> x0, starting transfers between devices: 16.4 us -> none  [the longest x1 7.33 us: local(): lax.all_to_all(sent, ('freq', 'lat'), split_axis=0, concat_axis=0, tiled=...]
    mul x4 -> x0, other arithmetic: 8.42 us -> none  [the longest x1 5.86 us: local(): odd = damped * jnp.sin(phase) * odd_sign]
    all_to_all x1 -> x0, blocking collectives: 8.39 us -> none  [local(): lax.all_to_all(jnp.stack(images, 1), 'freq', split_axis=0, concat_axis=0,...]
    all_to_all x3 -> x0, waiting for transfers between devices: 7.81 us -> none  [the longest x1 4.82 us: local(): lax.all_to_all(packed, 'lat', split_axis=0, concat_axis=0, tiled=True)]
    pallas_call x10 -> x1, Pallas kernels: 52.3 us -> 59.1 us  [local(): pl.pallas_call(functools.partial(program, cfg), out_shape=[jax.ShapeDtype...]
    reduce_sum x6 -> x0, other arithmetic: 3.05 us -> none  [the longest x1 1.18 us: local(): jnp.sum(((tile_id[:, None] == tile_id[None, :]) & (order[:, None] < order...]
    reshape x6 -> x0, local copies, waits for them, and re-layouts: 3.03 us -> none  [the longest x1 1.09 us: local(): coeffs = coeffs.reshape(2 * mode_rows, ny // TB * MODES)]
    unnamed x34 -> x4, local copies, waits for them, and re-layouts: 4.84 us -> 2.34 us
  transfers between devices with their start and end apart: 3 -> 0, of which waited for: 2 -> 0; matrix products, arithmetic and copies ran while one was open for 10% -> 0% of each run, Pallas kernels for 0% -> 0%
where the time goes in v1:
time: 63.6 us; the launch traced here: 62.7 us
  Pallas kernels  59.1 us (93%)
  local copies, waits for them, and re-layouts  2.34 us (4%)
  between operations  1.29 us (2%)
    pallas_call x1, Pallas kernels, local(): pl.pallas_call(functools.partial(program, cfg), out_shape=[jax.ShapeDtype...  59.1 us
    unnamed x4, local copies, waits for them, and re-layouts  2.34 us

profile of v1, /device:TPU:0, one launch (start us, length us, event | category | flops | bytes accessed | tf_op | source)
XLA Modules:
  0.0 62.7 jit_solution(7964615532972668863)
XLA Ops:
  1.3 59.1 %shard_map.122 = (f32[2,64,512]{2,1,0:T(8,128)}, f32[2,64,128]{2,1,0:T(8,128)}) custom-call(f32[2,4,1024]{2,1,0:T(4,128)} %spectra_ref.1, s32[1,1024]{1,0:T(1,128)} %bitcast.7, s32[1,1024]{1,0:T(1,128)} %bitcast.8, f32[2,1024]{1,0:T(2,128)} %offset_ref.1, f32[1,1024]{1,0:T(1,128)} %bitcast.9, f32[1]{0:T(128)S(6)} %copy.16.freq_ref, f32[2,8]{1,0:T(2,128)} %slow_ref.1, ...), custom_call_target="tpu_custom_call" | custom-call | tf_op jit(solution)/shard_map/pallas_call | solution.py:514
  60.4 0.0 copy-start
  60.4 1.7 %copy.17 = f32[2,1,64,512]{3,2,1,0:T(8,128)} copy(f32[2,1,64,512]{3,2,1,0:T(8,128)} %bitcast.6) | data formatting | bytes 524288
  62.1 0.0 copy-done
  62.1 0.6 %copy.18 = f32[2,64,128]{2,1,0:T(8,128)} copy(f32[2,64,128]{2,1,0:T(8,128)S(1)} %copy-done) | data formatting | bytes 131072
Async XLA Ops:
  60.4 1.7 %copy-start = (f32[2,64,128]{2,1,0:T(8,128)S(1)}, f32[2,64,128]{2,1,0:T(8,128)}, u32[]{:S(2)}) copy-start(f32[2,64,128]{2,1,0:T(8,128)} %get-tuple-element.11) | copy-start | bytes 196612

commit v2 on v1

v2 whole, which is shorter than its diff:
```python
import functools
import math

import jax
import jax.numpy as jnp
import numpy as np
from jax import lax
from jax.experimental import pallas as pl
from jax.experimental.pallas import tpu as pltpu
from jax.sharding import PartitionSpec as P

TB = 32
MODES = 8
CAP = 8
TERMS = MODES * MODES
REFS = 2

damping = 1.0
depth_step = 1.0

NN = (((1,), (0,)), ((), ()))
NT = (((1,), (1,)), ((), ()))
VMEM = pl.BlockSpec(memory_space=pltpu.VMEM)
SMEM = pl.BlockSpec(memory_space=pltpu.SMEM)
HBM = pl.BlockSpec(memory_space=pltpu.HBM)
MESH = pl.DeviceIdType.MESH


def two_parts(exact):
    high = exact.astype(jnp.bfloat16)
    low = (exact - high.astype(np.float64)).astype(jnp.bfloat16)
    return high, low


def hartley(length):
    at = np.arange(length)
    angle = 2.0 * math.pi / length * (at[:, None] * at[None, :] % length)
    return (np.cos(angle) + np.sin(angle)) / math.sqrt(length)


def half_tables(length):
    whole = hartley(length)[:, : length // 2]
    even, odd = whole[0::2], whole[1::2]
    return np.stack([np.stack(two_parts(one), 0) for one in (even, odd, odd.T)], 0)


def mode_tables(length):
    cosines = np.cos(math.pi * np.arange(MODES)[:, None] * (np.arange(TB)[None, :] + 0.5) / TB)
    count = length // TB // 2
    fold = np.zeros((count, MODES, length))
    for tile in range(count):
        fold[tile, :, tile * TB : (tile + 1) * TB] = cosines
    whole = fold.reshape(count * MODES, length) @ hartley(length)
    left, right = [], []
    for parity in range(2):
        high, low = two_parts(whole[:, parity::2])
        right.append(np.concatenate([high, high, low], 0))
        left.append(np.concatenate([high.T, low.T, high.T], 1))
    return np.stack(left, 0), np.stack(right, 0)


def split2(x):
    high = x.astype(jnp.bfloat16)
    return high, (x - high.astype(jnp.float32)).astype(jnp.bfloat16)


def dot(a, b, dims=NN):
    return lax.dot_general(a, b, dims, preferred_element_type=jnp.float32)


def dot3(a, b, dims=NN):
    return dot(a[0], b[0], dims) + (dot(a[0], b[1], dims) + dot(a[1], b[0], dims))


def series(value, first, count):
    total = jnp.full(value.shape, 1.0 / math.factorial(2 * (count - 1) + first), jnp.float32)
    for n in range(count - 2, -1, -1):
        total = 1.0 / math.factorial(2 * n + first) - value * total
    return total


def cosine_of(cell):
    angle = (0.5 * TB - (cell + 0.5)) * (math.pi / TB)
    return angle * series(angle * angle, 1, 9)


def propagator(wave_squared, kx, ky):
    vertical = wave_squared - kx * kx - ky * ky
    root = jnp.sqrt(jnp.abs(vertical)) * depth_step
    squared = root * root
    moving = vertical > 0.0
    even = jnp.where(moving, series(squared, 0, 10), jnp.exp(-root))
    odd = jnp.where(moving, root * series(squared, 1, 10), 0.0)
    return even, odd


def signed(place, length):
    half = length // 2
    index = 2 * lax.rem(place, half) + lax.div(place, half)
    return 2.0 * math.pi / length * jnp.where(index >= half, index - length, index).astype(jnp.float32)


def iota(shape, axis):
    return lax.broadcasted_iota(jnp.int32, shape, axis)


def program(
    cfg,
    spectra_hbm,
    tile_hbm,
    bin_hbm,
    offset_hbm,
    weight_hbm,
    freq_ref,
    slow_ref,
    vel_hbm,
    hart_hbm,
    modes_x_hbm,
    modes_y_hbm,
    wave_ref,
    image_ref,
    spectra_ref,
    tile_ref,
    bin_ref,
    offset_ref,
    weight_ref,
    hart,
    modes_x,
    modes_y,
    vel_first,
    vel_last,
    route_out,
    route_in,
    system,
    coef_out,
    coef_in,
    wide_even,
    wide_odd,
    band_even,
    band_odd,
    along_first,
    across_first,
    along_last,
    across_last,
    fwd_out,
    fwd_in,
    back_out,
    back_in,
    image_out,
    image_in,
    trace_sem,
    table_sem,
    route_sent,
    route_got,
    coef_sent,
    coef_got,
    vel_sem,
    fwd_sent,
    fwd_got,
    back_sent,
    back_got,
    image_sent,
    image_got,
):
    F, L, tiles, nx, ny, rows, data_rows, padded, nvel = cfg
    devices = F * L
    group = L // 2
    half_x, half_y = nx // 2, ny // 2
    band = ny // group
    slots = tiles * CAP
    per_group = nvel // REFS
    me_f = lax.axis_index("freq")
    me_l = lax.axis_index("lat")
    me = me_l * F + me_f
    side = lax.div(me_l, group)
    seat = lax.rem(me_l, group)

    barrier = pltpu.get_barrier_semaphore()

    def partner_of(at):
        step = devices // 2 + (1 - 2 * lax.rem(at, 2)) * lax.div(at, 2)
        other = lax.rem(me + step, devices)
        return other, {"freq": lax.rem(other, F), "lat": lax.div(other, F)}

    def greet(at, carry):
        _, device = partner_of(at)
        pl.semaphore_signal(barrier, inc=1, device_id=device, device_id_type=MESH)
        return carry

    inputs = [
        pltpu.make_async_copy(src, dst, trace_sem.at[at])
        for at, (src, dst) in enumerate(
            [
                (tile_hbm, tile_ref),
                (bin_hbm, bin_ref),
                (offset_hbm, offset_ref),
                (weight_hbm, weight_ref),
                (spectra_hbm, spectra_ref),
            ]
        )
    ]
    for load in inputs:
        load.start()
    lax.fori_loop(1, devices, greet, 0)
    loads = [
        pltpu.make_async_copy(src, dst, table_sem.at[at])
        for at, (src, dst) in enumerate(
            [
                (vel_hbm.at[0], vel_first.at[side]),
                (vel_hbm.at[1], vel_last),
                (modes_x_hbm, modes_x),
                (modes_y_hbm, modes_y),
                (hart_hbm, hart),
            ]
        )
    ]
    for load in loads:
        load.start()
    for load in inputs:
        load.wait()

    count = tile_ref.shape[1]
    width = 128
    tile = tile_ref[...]
    columns = [
        jnp.transpose(jnp.broadcast_to(tile[:, at : at + width], (width, width)))
        for at in range(0, count, width)
    ]
    earlier = iota((width, width), 0) < iota((width, width), 1)
    ranks = []
    for at in range(count // width):
        row = jnp.broadcast_to(tile[:, at * width : (at + 1) * width], (width, width))
        same = jnp.where((columns[at] == row) & earlier, 1, 0)
        for before in range(at):
            same = same + jnp.where(columns[before] == row, 1, 0)
        ranks.append(jnp.sum(same, 0, keepdims=True))
    rank = jnp.concatenate(ranks, 1)
    turned = lax.rem(lax.rem(tile, tiles) + me, tiles)
    slot = lax.div(tile, tiles) * slots + turned * CAP + rank

    cell = bin_ref[...]
    root_weight = jnp.sqrt(weight_ref[...])
    cell_x = lax.div(cell, TB).astype(jnp.float32) + offset_ref[0:1, :]
    cell_y = lax.rem(cell, TB).astype(jnp.float32) + offset_ref[1:2, :]
    feats = jnp.concatenate(
        [spectra_ref[0] * root_weight, spectra_ref[1] * root_weight]
        + [root_weight, cosine_of(cell_x), cosine_of(cell_y)]
        + [jnp.zeros((padded - data_rows - 3, count), jnp.float32)],
        0,
    )
    high = feats.astype(jnp.bfloat16)
    rest = feats - high.astype(jnp.float32)
    middle = rest.astype(jnp.bfloat16)
    low = (rest - middle.astype(jnp.float32)).astype(jnp.bfloat16)
    parts = jnp.concatenate([high, middle, low], 0)
    wide = 256
    for at in range(0, devices * slots, wide):
        places = iota((wide, count), 0) + at
        chosen = jnp.where(places == slot, 1.0, 0.0).astype(jnp.bfloat16)
        got = dot(parts, chosen, NT)
        got = got[:padded] + got[padded : 2 * padded] + got[2 * padded :]
        for piece in range(wide // slots):
            route_out[at // slots + piece] = got[:, piece * slots : (piece + 1) * slots]

    pl.semaphore_wait(barrier, devices - 1)

    def spread(out, into, sent, landed):
        def copy_of(at):
            other, device = partner_of(at)
            return pltpu.make_async_remote_copy(
                src_ref=out.at[other] if out.shape[0] == devices else out.at[lax.rem(other, F)],
                dst_ref=into.at[me],
                send_sem=sent.at[at],
                recv_sem=landed.at[at],
                device_id=device,
                device_id_type=MESH,
            )

        def start(at, carry):
            copy_of(at).start()
            return carry

        def arrive(at, carry):
            copy_of(at).wait_recv()
            return carry

        def leave(at, carry):
            copy_of(at).wait_send()
            return carry

        lax.fori_loop(1, devices, start, 0)
        return (
            lambda: lax.fori_loop(1, devices, arrive, 0),
            lambda: lax.fori_loop(1, devices, leave, 0),
        )

    arrive, leave_route = spread(route_out, route_in, route_sent, route_got)
    route_in[pl.ds(me, 1)] = route_out[pl.ds(me, 1)]

    frequency = freq_ref[0]
    waves = []
    for depth_at in range(2):
        squares = []
        for g in range(REFS):
            total = slow_ref[depth_at, g * per_group]
            for i in range(1, per_group):
                total = total + slow_ref[depth_at, g * per_group + i]
            reference = total * (1.0 / per_group)
            squares.append((reference, (frequency * reference) * (frequency * reference)))
        waves.append(squares)

    chunk = 8

    def wide_tables(at, carry):
        first = pl.multiple_of(at * chunk, chunk)
        kx = signed(iota((chunk, ny), 0) + first, nx)
        ky = signed(iota((chunk, ny), 1), ny)
        for g in range(REFS):
            even, odd = propagator(waves[0][g][1], kx, ky)
            wide_even[g, pl.ds(first, chunk), :] = even
            wide_odd[g, pl.ds(first, chunk), :] = odd
        return carry

    lax.fori_loop(0, nx // chunk, wide_tables, 0)
    for load in loads:
        load.wait()
    arrive()

    mirror = pltpu.make_async_remote_copy(
        src_ref=vel_first.at[side],
        dst_ref=vel_first.at[side],
        send_sem=vel_sem.at[0],
        recv_sem=vel_sem.at[1],
        device_id={"lat": lax.rem(me_l + group, L)},
        device_id_type=MESH,
    )
    mirror.start()

    group_at = lax.div(iota((padded, slots), 1), CAP)
    eye = jnp.where(iota((TERMS, TERMS + data_rows), 0) == iota((TERMS, TERMS + data_rows), 1), damping, 0.0)

    def chebyshev(cosine):
        terms = [jnp.ones_like(cosine), cosine]
        for _ in range(MODES - 2):
            terms.append(2.0 * cosine * terms[-1] - terms[-2])
        return terms

    for t in range(tiles):
        pieces = []
        for first in range(0, devices, tiles):
            picked = route_in[first]
            for i in range(1, tiles):
                picked = jnp.where(group_at == (t + i) % tiles, route_in[first + i], picked)
            pieces.append(picked)
        got = jnp.concatenate(pieces, 1)
        scale = got[data_rows : data_rows + 1]
        along_x = chebyshev(got[data_rows + 1 : data_rows + 2])
        along_y = jnp.concatenate(chebyshev(got[data_rows + 2 : data_rows + 3]), 0)
        basis = jnp.concatenate([(term * scale) * along_y for term in along_x], 0)
        right = jnp.concatenate([basis, got[:data_rows]], 0)
        system[t] = eye + lax.dot_general(
            basis, right, NT, preferred_element_type=jnp.float32, precision=lax.Precision.HIGHEST
        )
    for k in range(TERMS):
        row = system[:, k : k + 1, :]
        scaled = row * (1.0 / row[:, :, k : k + 1])
        whole = system[...]
        system[...] = whole - whole[:, :, k : k + 1] * scaled
        system[:, k : k + 1, :] = scaled
    solved = [jnp.transpose(system[t])[TERMS:] for t in range(tiles)]
    for a in range(MODES):
        line = jnp.concatenate([one[:, a * MODES : (a + 1) * MODES] for one in solved], 1)
        for part in range(2):
            for f in range(F):
                at = part * F + f
                coef_out[f, part, a : a + 1, :] = line[at : at + 1]

    arrive, leave_coef = spread(coef_out, coef_in, coef_sent, coef_got)
    coef_in[pl.ds(me, 1)] = coef_out[pl.ds(me_f, 1)]

    ky = signed(seat * band + iota((chunk, band), 1), ny)

    def band_tables(at, carry):
        first = pl.multiple_of(at * chunk, chunk)
        kx = signed(iota((chunk, band), 0) + first, nx)
        for g in range(REFS):
            even, odd = propagator(waves[1][g][1], kx, ky)
            band_even[g, pl.ds(first, chunk), :] = even
            band_odd[g, pl.ds(first, chunk), :] = odd
        return carry

    lax.fori_loop(0, nx // chunk, band_tables, 0)

    def split_step(depth_at, velocity):
        cosine = jnp.zeros(velocity.shape, jnp.float32)
        sine = jnp.zeros(velocity.shape, jnp.float32)
        for i in range(nvel):
            shift = slow_ref[depth_at, i] - waves[depth_at][i // per_group][0]
            angle = jnp.full((8, 128), frequency * shift * depth_step, jnp.float32)
            squared = angle * angle
            cosine_i = series(squared, 0, 9)[0:1, 0:1]
            sine_i = (angle * series(squared, 1, 9))[0:1, 0:1]
            cosine = jnp.where(velocity == i, cosine_i, cosine)
            sine = jnp.where(velocity == i, sine_i, sine)
        return cosine, sine

    along_last[...], across_last[...] = split_step(1, vel_last[...])
    mirror.wait_recv()
    for one in range(2):
        along_first[one], across_first[one] = split_step(0, vel_first[one])
    arrive()

    def part_of(which):
        return hart[which, 0], hart[which, 1]

    even_k, odd_k, odd_k_t = part_of(0), part_of(1), part_of(2)

    def from_modes_of(parts):
        return jnp.concatenate([parts[0], parts[1], parts[0]], 1)

    per_row = (ny // TB) // tiles
    tile_rows = nx // TB
    mode_rows = tile_rows // 2 * MODES
    mode_columns = ny // TB // 2 * MODES
    sums, differences = [], []
    for part in range(2):
        lines = [
            jnp.concatenate([coef_in[tile_row * per_row + j, part] for j in range(per_row)], 1)
            for tile_row in range(tile_rows)
        ]
        upper = jnp.concatenate(lines[: tile_rows // 2], 0)
        lower = jnp.concatenate(lines[tile_rows // 2 :], 0)
        for one in (upper + lower, upper - lower):
            left, right = one[:, :mode_columns], one[:, mode_columns:]
            sums.append(left + right)
            differences.append(left - right)
    spread_y = [
        dot(from_modes_of(split2(jnp.concatenate(one, 0))), modes_y[parity])
        for parity, one in enumerate((sums, differences))
    ]
    seat_rows = pl.ds(pl.multiple_of(seat * rows, rows), rows)
    made = [[None, None] for _ in range(REFS)]
    for parity in range(2):
        picked = [
            one[(2 * p + parity) * mode_rows : (2 * p + parity + 1) * mode_rows]
            for p in range(2)
            for one in spread_y
        ]
        high, low = split2(jnp.concatenate(picked, 1))
        spectrum = dot(modes_x[parity], jnp.concatenate([high, high, low], 0))
        real, imag = spectrum[:, :ny], spectrum[:, ny:]
        which = 0 if parity == 0 else 2
        own_high, own_low = hart[which, 0, seat_rows, :], hart[which, 1, seat_rows, :]
        both = jnp.concatenate([own_high, own_low], 0)
        part = slice(parity * half_x, (parity + 1) * half_x)
        for g in range(REFS):
            even, odd = wide_even[g, part, :], wide_odd[g, part, :]
            moved = split2(jnp.concatenate([real * even - imag * odd, real * odd + imag * even], 1))
            back = dot(both, moved[0])
            made[g][parity] = back[:rows] + (back[rows:] + dot(own_high, moved[1]))
    pieces = []
    for g in range(REFS):
        slabs = (made[g][0] + made[g][1], made[g][0] - made[g][1])
        for p in range(2):
            pieces += [slab[:, p * ny : (p + 1) * ny] for slab in slabs]

    def inverse_y(x):
        u = dot3(split2(x[:, :half_y]), even_k)
        v = dot3(split2(x[:, half_y:]), odd_k)
        return jnp.concatenate([u + v, u - v], 1)

    def choose(made, velocity):
        real, imag = made[0]
        for g in range(1, REFS):
            chosen = velocity >= g * per_group
            real = jnp.where(chosen, made[g][0], real)
            imag = jnp.where(chosen, made[g][1], imag)
        return real, imag

    image_piece = ny // F

    def send_image(depth_at, real):
        for f in range(F):
            image_out[depth_at, f] = real[:, f * image_piece : (f + 1) * image_piece]
        copies = []
        for step in range(1, F):
            other = lax.rem(me_f + step, F)
            copies.append(
                pltpu.make_async_remote_copy(
                    src_ref=image_out.at[depth_at, other],
                    dst_ref=image_in.at[depth_at, me_f],
                    send_sem=image_sent.at[depth_at, step],
                    recv_sem=image_got.at[depth_at, step],
                    device_id={"freq": other},
                    device_id_type=MESH,
                )
            )
        for copy in copies:
            copy.start()
        image_in[depth_at, pl.ds(me_f, 1)] = image_out[depth_at, pl.ds(me_f, 1)]
        return copies

    def exchange(at, out, into, sent, landed):
        copies = []
        for step in range(1, group):
            other = lax.rem(seat + step, group)
            copies.append(
                pltpu.make_async_remote_copy(
                    src_ref=out.at[at, other],
                    dst_ref=into.at[at, seat],
                    send_sem=sent.at[at, step],
                    recv_sem=landed.at[at, step],
                    device_id={"lat": side * group + other},
                    device_id_type=MESH,
                )
            )
        for copy in copies:
            copy.start()
        into[at, pl.ds(seat, 1)] = out[at, pl.ds(seat, 1)]
        return copies

    field = inverse_y(jnp.concatenate(pieces, 0))
    two = 2 * rows
    real, imag = choose(
        [(field[2 * g * two : (2 * g + 1) * two], field[(2 * g + 1) * two : (2 * g + 2) * two]) for g in range(REFS)],
        vel_first[...].reshape(two, ny),
    )
    cosine, sine = along_first[...].reshape(two, ny), across_first[...].reshape(two, ny)
    real, imag = real * cosine - imag * sine, real * sine + imag * cosine
    forward = []
    for p, one in enumerate((real, imag)):
        left, right = one[:, :half_y], one[:, half_y:]
        line = jnp.concatenate(
            [dot3(split2(left + right), even_k), dot3(split2(left - right), odd_k_t)], 1
        )
        for dst in range(group):
            fwd_out[p, dst] = line[:, dst * band : (dst + 1) * band].reshape(2, rows, band)
        forward.append(exchange(p, fwd_out, fwd_in, fwd_sent, fwd_got))
    first_image = send_image(0, jnp.where(side == 0, real[:rows], real[rows:]))

    spectrum = []
    for p in range(2):
        for copy in forward[p]:
            copy.wait_recv()
        upper = jnp.concatenate([fwd_in[p, src, 0] for src in range(group)], 0)
        lower = jnp.concatenate([fwd_in[p, src, 1] for src in range(group)], 0)
        lines = []
        for one, table in ((upper + lower, even_k), (upper - lower, odd_k)):
            high, low = split2(one)
            line = dot(table[0], jnp.concatenate([high, low], 1))
            lines.append(line[:, :band] + (line[:, band:] + dot(table[1], high)))
        spectrum.append(lines)
    turn = (1 - 2 * side).astype(jnp.float32)
    backward = []
    for g in range(REFS):
        sides = []
        for parity, table in enumerate((even_k, odd_k_t)):
            part = slice(parity * half_x, (parity + 1) * half_x)
            even, odd = band_even[g, part, :], band_odd[g, part, :]
            real, imag = spectrum[0][parity], spectrum[1][parity]
            moved = jnp.concatenate([real * even - imag * odd, real * odd + imag * even], 1)
            sides.append(dot3(table, split2(moved)))
        back_out[g] = (sides[0] + turn * sides[1]).reshape(group, rows, 2 * band)
        backward.append(exchange(g, back_out, back_in, back_sent, back_got))
    made = []
    for g in range(REFS):
        for copy in backward[g]:
            copy.wait_recv()
        lines = [
            jnp.concatenate([back_in[g, src, :, p * band : (p + 1) * band] for src in range(group)], 1)
            for p in range(2)
        ]
        field = inverse_y(jnp.concatenate(lines, 0))
        made.append((field[:rows], field[rows:]))
    real, imag = choose(made, vel_last[...])
    cosine, sine = along_last[...], across_last[...]
    moved = real * cosine - imag * sine
    last_image = send_image(1, moved)
    wave_ref[0] = moved
    wave_ref[1] = real * sine + imag * cosine

    leave_route()
    leave_coef()
    mirror.wait_send()
    for copies in forward + backward:
        for copy in copies:
            copy.wait_send()
    for depth_at, copies in enumerate((first_image, last_image)):
        for copy in copies:
            copy.wait()
        total = image_in[depth_at, 0]
        for f in range(1, F):
            total = total + image_in[depth_at, f]
        image_ref[depth_at] = total


def stay(x):
    return pltpu.with_memory_space_constraint(x, pltpu.HBM)


def local(spectra, tile_route, bin_in_tile, trace_offset, weights, frequency, slowness, vel_index):
    F = lax.axis_size("freq")
    L = lax.axis_size("lat")
    devices = F * L
    steps, rows, ny = vel_index.shape
    assert steps == 2
    nx = rows * L
    tiles = (nx // TB) * (ny // TB) // devices
    slots = tiles * CAP
    count = spectra.shape[2]
    data_rows = 2 * spectra.shape[1]
    padded = -(-(data_rows + 3) // 16) * 16
    group = L // 2
    band = ny // group
    nvel = slowness.shape[1]
    cfg = (F, L, tiles, nx, ny, rows, data_rows, padded, nvel)

    hart = jnp.asarray(half_tables(nx))
    modes_x, modes_y = (jnp.asarray(one) for one in mode_tables(nx))

    f32, bf16, i32 = jnp.float32, jnp.bfloat16, jnp.int32
    dma = pltpu.SemaphoreType.DMA
    wave, image = pl.pallas_call(
        functools.partial(program, cfg),
        out_shape=[
            jax.ShapeDtypeStruct((2, rows, ny), f32),
            jax.ShapeDtypeStruct((2, rows, ny // F), f32),
        ],
        in_specs=[HBM] * 5 + [SMEM] * 2 + [HBM] * 4,
        out_specs=[VMEM, VMEM],
        scratch_shapes=[
            pltpu.VMEM(spectra.shape, f32),
            pltpu.VMEM((1, count), i32),
            pltpu.VMEM((1, count), i32),
            pltpu.VMEM((2, count), f32),
            pltpu.VMEM((1, count), f32),
            pltpu.VMEM(hart.shape, bf16),
            pltpu.VMEM(modes_x.shape, bf16),
            pltpu.VMEM(modes_y.shape, bf16),
            pltpu.VMEM((2, rows, ny), i32),
            pltpu.VMEM((rows, ny), i32),
            pltpu.VMEM((devices, padded, slots), f32),
            pltpu.VMEM((devices, padded, slots), f32),
            pltpu.VMEM((tiles, TERMS, TERMS + data_rows), f32),
            pltpu.VMEM((F, 2, MODES, tiles * MODES), f32),
            pltpu.VMEM((devices, 2, MODES, tiles * MODES), f32),
            pltpu.VMEM((REFS, nx, ny), f32),
            pltpu.VMEM((REFS, nx, ny), f32),
            pltpu.VMEM((REFS, nx, band), f32),
            pltpu.VMEM((REFS, nx, band), f32),
            pltpu.VMEM((2, rows, ny), f32),
            pltpu.VMEM((2, rows, ny), f32),
            pltpu.VMEM((rows, ny), f32),
            pltpu.VMEM((rows, ny), f32),
            pltpu.VMEM((2, group, 2, rows, band), f32),
            pltpu.VMEM((2, group, 2, rows, band), f32),
            pltpu.VMEM((REFS, group, rows, 2 * band), f32),
            pltpu.VMEM((REFS, group, rows, 2 * band), f32),
            pltpu.VMEM((2, F, rows, ny // F), f32),
            pltpu.VMEM((2, F, rows, ny // F), f32),
            dma((5,)),
            dma((5,)),
            dma((devices,)),
            dma((devices,)),
            dma((devices,)),
            dma((devices,)),
            dma((2,)),
            dma((2, group)),
            dma((2, group)),
            dma((REFS, group)),
            dma((REFS, group)),
            dma((2, F)),
            dma((2, F)),
        ],
        compiler_params=pltpu.CompilerParams(
            collective_id=0, has_side_effects=True, vmem_limit_bytes=40 << 20
        ),
    )(
        *map(stay, (spectra, tile_route.reshape(1, count), bin_in_tile.reshape(1, count))),
        *map(stay, (trace_offset, weights.reshape(1, count))),
        frequency,
        stay(slowness),
        *map(stay, (vel_index, hart, modes_x, modes_y)),
    )
    return wave[:, None], image


def solution(mesh):
    return jax.shard_map(
        local,
        mesh=mesh,
        in_specs=(
            P(None, None, ("freq", "lat")),
            P(("freq", "lat"), None),
            P(("freq", "lat")),
            P(None, ("freq", "lat")),
            P(("freq", "lat")),
            P("freq"),
            P(),
            P(None, "lat", None),
        ),
        out_specs=(P(None, "freq", "lat", None), P(None, "lat", "freq")),
        check_vma=False,
    )
```

time: 63.6 us -> 57.2 us (0.90); the launches traced: 62.7 us -> 57 us
  Pallas kernels: 59.1 us -> 54.4 us
  local copies, waits for them, and re-layouts: 2.34 us -> 1.33 us
    pallas_call x1, Pallas kernels: 59.1 us -> 54.4 us  [local(): pl.pallas_call(functools.partial(program, cfg), out_shape=[jax.ShapeDtype...]
    unnamed x4 -> x2, local copies, waits for them, and re-layouts: 2.34 us -> 1.33 us
where the time goes in v2:
time: 57.2 us; the launch traced here: 57 us
  Pallas kernels  54.4 us (95%)
  local copies, waits for them, and re-layouts  1.33 us (2%)
  between operations  1.29 us (2%)
    pallas_call x1, Pallas kernels, local(): pl.pallas_call(functools.partial(program, cfg), out_shape=[jax.ShapeDtype...  54.4 us
    unnamed x2, local copies, waits for them, and re-layouts  1.33 us

profile of v2, /device:TPU:0, one launch (start us, length us, event | category | flops | bytes accessed | tf_op | source)
XLA Modules:
  0.0 57.0 jit_solution(8953237286788840530)
XLA Ops:
  1.3 54.4 %shard_map.122 = (f32[2,64,512]{2,1,0:T(8,128)S(1)}, f32[2,64,128]{2,1,0:T(8,128)S(1)}) custom-call(f32[2,4,1024]{2,1,0:T(4,128)} %spectra_hbm.1, s32[1,1024]{1,0:T(1,128)} %bitcast.7, s32[1,1024]{1,0:T(1,128)} %bitcast.8, f32[2,1024]{1,0:T(2,128)} %offset_hbm.1, f32[1,1024]{1,0:T(1,128)} %bitcast.9, f32[1]{0:T(128)S(6)} %copy.16.freq_ref, f32[2,8]{1,0:T(2,128)} %slow_ref.1, ...), custom_call_target="tpu_custom_call" | custom-call | tf_op jit(solution)/shard_map/pallas_call | solution.py:623
  55.7 0.7 %copy.17 = f32[2,1,64,512]{3,2,1,0:T(8,128)} copy(f32[2,1,64,512]{3,2,1,0:T(8,128)S(1)} %bitcast.6) | data formatting | bytes 524288
  56.4 0.6 %copy.18 = f32[2,64,128]{2,1,0:T(8,128)} copy(f32[2,64,128]{2,1,0:T(8,128)S(1)} %get-tuple-element.11) | data formatting | bytes 131072

commit v3 on v2

--- a/solution.py
+++ b/solution.py
@@ -178,8 +178,7 @@
     barrier = pltpu.get_barrier_semaphore()
 
     def partner_of(at):
-        step = devices // 2 + (1 - 2 * lax.rem(at, 2)) * lax.div(at, 2)
-        other = lax.rem(me + step, devices)
+        other = lax.rem(me + at, devices)
         return other, {"freq": lax.rem(other, F), "lat": lax.div(other, F)}
 
     def greet(at, carry):
@@ -260,7 +259,8 @@
         got = dot(parts, chosen, NT)
         got = got[:padded] + got[padded : 2 * padded] + got[2 * padded :]
         for piece in range(wide // slots):
-            route_out[at // slots + piece] = got[:, piece * slots : (piece + 1) * slots]
+            block = got[:, piece * slots : (piece + 1) * slots]
+            route_out[at // slots + piece] = jnp.concatenate([block[:data_rows], block[data_rows:]], 1)
 
     pl.semaphore_wait(barrier, devices - 1)
 
@@ -336,7 +336,7 @@
     )
     mirror.start()
 
-    group_at = lax.div(iota((padded, slots), 1), CAP)
+    group_at = lax.div(lax.rem(iota((data_rows, 2 * slots), 1), slots), CAP)
     eye = jnp.where(iota((TERMS, TERMS + data_rows), 0) == iota((TERMS, TERMS + data_rows), 1), damping, 0.0)
 
     def chebyshev(cosine):
@@ -352,12 +352,13 @@
             for i in range(1, tiles):
                 picked = jnp.where(group_at == (t + i) % tiles, route_in[first + i], picked)
             pieces.append(picked)
-        got = jnp.concatenate(pieces, 1)
-        scale = got[data_rows : data_rows + 1]
-        along_x = chebyshev(got[data_rows + 1 : data_rows + 2])
-        along_y = jnp.concatenate(chebyshev(got[data_rows + 2 : data_rows + 3]), 0)
+        data = jnp.concatenate([piece[:, :slots] for piece in pieces], 1)
+        place = jnp.concatenate([piece[:8, slots:] for piece in pieces], 1)
+        scale = place[0:1]
+        along_x = chebyshev(place[1:2])
+        along_y = jnp.concatenate(chebyshev(place[2:3]), 0)
         basis = jnp.concatenate([(term * scale) * along_y for term in along_x], 0)
-        right = jnp.concatenate([basis, got[:data_rows]], 0)
+        right = jnp.concatenate([basis, data], 0)
         system[t] = eye + lax.dot_general(
             basis, right, NT, preferred_element_type=jnp.float32, precision=lax.Precision.HIGHEST
         )
@@ -368,12 +369,13 @@
         system[...] = whole - whole[:, :, k : k + 1] * scaled
         system[:, k : k + 1, :] = scaled
     solved = [jnp.transpose(system[t])[TERMS:] for t in range(tiles)]
+    width = tiles * MODES
     for a in range(MODES):
         line = jnp.concatenate([one[:, a * MODES : (a + 1) * MODES] for one in solved], 1)
         for part in range(2):
             for f in range(F):
                 at = part * F + f
-                coef_out[f, part, a : a + 1, :] = line[at : at + 1]
+                coef_out[f, a : a + 1, part * width : (part + 1) * width] = line[at : at + 1]
 
     arrive, leave_coef = spread(coef_out, coef_in, coef_sent, coef_got)
     coef_in[pl.ds(me, 1)] = coef_out[pl.ds(me_f, 1)]
@@ -425,7 +427,13 @@
     sums, differences = [], []
     for part in range(2):
         lines = [
-            jnp.concatenate([coef_in[tile_row * per_row + j, part] for j in range(per_row)], 1)
+            jnp.concatenate(
+                [
+                    coef_in[tile_row * per_row + j, :, part * width : (part + 1) * width]
+                    for j in range(per_row)
+                ],
+                1,
+            )
             for tile_row in range(tile_rows)
         ]
         upper = jnp.concatenate(lines[: tile_rows // 2], 0)
@@ -609,7 +617,7 @@
     slots = tiles * CAP
     count = spectra.shape[2]
     data_rows = 2 * spectra.shape[1]
-    padded = -(-(data_rows + 3) // 16) * 16
+    padded = 2 * data_rows
     group = L // 2
     band = ny // group
     nvel = slowness.shape[1]
@@ -639,11 +647,11 @@
             pltpu.VMEM(modes_y.shape, bf16),
             pltpu.VMEM((2, rows, ny), i32),
             pltpu.VMEM((rows, ny), i32),
-            pltpu.VMEM((devices, padded, slots), f32),
-            pltpu.VMEM((devices, padded, slots), f32),
+            pltpu.VMEM((devices, data_rows, 2 * slots), f32),
+            pltpu.VMEM((devices, data_rows, 2 * slots), f32),
             pltpu.VMEM((tiles, TERMS, TERMS + data_rows), f32),
-            pltpu.VMEM((F, 2, MODES, tiles * MODES), f32),
-            pltpu.VMEM((devices, 2, MODES, tiles * MODES), f32),
+            pltpu.VMEM((F, MODES, 2 * tiles * MODES), f32),
+            pltpu.VMEM((devices, MODES, 2 * tiles * MODES), f32),
             pltpu.VMEM((REFS, nx, ny), f32),
             pltpu.VMEM((REFS, nx, ny), f32),
             pltpu.VMEM((REFS, nx, band), f32),

time: 57.2 us -> 52.5 us (0.918)
  Pallas kernels: 54.4 us -> 49.6 us
    pallas_call x1, Pallas kernels: 54.4 us -> 49.6 us  [local(): pl.pallas_call(functools.partial(program, cfg), out_shape=[jax.ShapeDtype...]
where the time goes in v3:
time: 52.5 us; the launch traced here: 52.2 us
  Pallas kernels  49.6 us (94%)
  local copies, waits for them, and re-layouts  1.33 us (3%)
  between operations  1.29 us (2%)
    pallas_call x1, Pallas kernels, local(): pl.pallas_call(functools.partial(program, cfg), out_shape=[jax.ShapeDtype...  49.6 us
    unnamed x2, local copies, waits for them, and re-layouts  1.33 us

profile of v3, /device:TPU:0, one launch (start us, length us, event | category | flops | bytes accessed | tf_op | source)
XLA Modules:
  0.0 52.2 jit_solution(6369351899671054533)
XLA Ops:
  1.3 49.6 %shard_map.122 = (f32[2,64,512]{2,1,0:T(8,128)S(1)}, f32[2,64,128]{2,1,0:T(8,128)S(1)}) custom-call(f32[2,4,1024]{2,1,0:T(4,128)} %spectra_hbm.1, s32[1,1024]{1,0:T(1,128)} %bitcast.7, s32[1,1024]{1,0:T(1,128)} %bitcast.8, f32[2,1024]{1,0:T(2,128)} %offset_hbm.1, f32[1,1024]{1,0:T(1,128)} %bitcast.9, f32[1]{0:T(128)S(6)} %copy.16.freq_ref, f32[2,8]{1,0:T(2,128)} %slow_ref.1, ...), custom_call_target="tpu_custom_call" | custom-call | tf_op jit(solution)/shard_map/pallas_call | solution.py:631
  50.9 0.7 %copy.17 = f32[2,1,64,512]{3,2,1,0:T(8,128)} copy(f32[2,1,64,512]{3,2,1,0:T(8,128)S(1)} %bitcast.6) | data formatting | bytes 524288
  51.6 0.6 %copy.18 = f32[2,64,128]{2,1,0:T(8,128)} copy(f32[2,64,128]{2,1,0:T(8,128)S(1)} %get-tuple-element.11) | data formatting | bytes 131072

commit v4 on v3

--- a/solution.py
+++ b/solution.py
@@ -38,23 +38,32 @@
     return (np.cos(angle) + np.sin(angle)) / math.sqrt(length)
 
 
+def orders(length):
+    at = np.arange(length // 4)
+    even = np.concatenate([2 * at, (length - 2 * at) % length])
+    even[length // 4] = length // 2
+    return even, np.concatenate([2 * at + 1, length - 1 - 2 * at])
+
+
 def half_tables(length):
     whole = hartley(length)[:, : length // 2]
-    even, odd = whole[0::2], whole[1::2]
-    return np.stack([np.stack(two_parts(one), 0) for one in (even, odd, odd.T)], 0)
-
-
-def mode_tables(length):
+    even, odd = (whole[order] for order in orders(length))
+    return np.stack([np.stack(two_parts(one), 0) for one in (even, even.T, odd, odd.T)], 0)
+
+
+def mode_tables(length, inner):
     cosines = np.cos(math.pi * np.arange(MODES)[:, None] * (np.arange(TB)[None, :] + 0.5) / TB)
     count = length // TB // 2
     fold = np.zeros((count, MODES, length))
     for tile in range(count):
         fold[tile, :, tile * TB : (tile + 1) * TB] = cosines
-    whole = fold.reshape(count * MODES, length) @ hartley(length)
+    whole = fold @ hartley(length)
+    turned = whole.reshape(count, MODES // inner, inner, length).swapaxes(1, 2)
     left, right = [], []
-    for parity in range(2):
-        high, low = two_parts(whole[:, parity::2])
+    for order in orders(length):
+        high, low = two_parts(whole.reshape(count * MODES, length)[:, order])
         right.append(np.concatenate([high, high, low], 0))
+        high, low = two_parts(turned.reshape(count * MODES, length)[:, order])
         left.append(np.concatenate([high.T, low.T, high.T], 1))
     return np.stack(left, 0), np.stack(right, 0)
 
@@ -94,10 +103,15 @@
     return even, odd
 
 
-def signed(place, length):
-    half = length // 2
-    index = 2 * lax.rem(place, half) + lax.div(place, half)
-    return 2.0 * math.pi / length * jnp.where(index >= half, index - length, index).astype(jnp.float32)
+def wave_number(place, length):
+    half, quarter = length // 2, length // 4
+    index = 2 * lax.rem(place, quarter) + lax.div(place, half)
+    index = jnp.where(place == quarter, half, index)
+    return 2.0 * math.pi / length * index.astype(jnp.float32)
+
+
+def take_lanes(x, index):
+    return jnp.take_along_axis(x, index, axis=1, mode="promise_in_bounds")
 
 
 def iota(shape, axis):
@@ -112,7 +126,7 @@
     offset_hbm,
     weight_hbm,
     freq_ref,
-    slow_ref,
+    slow_hbm,
     vel_hbm,
     hart_hbm,
     modes_x_hbm,
@@ -124,6 +138,7 @@
     bin_ref,
     offset_ref,
     weight_ref,
+    slow_ref,
     hart,
     modes_x,
     modes_y,
@@ -131,7 +146,6 @@
     vel_last,
     route_out,
     route_in,
-    system,
     coef_out,
     coef_in,
     wide_even,
@@ -186,6 +200,7 @@
         pl.semaphore_signal(barrier, inc=1, device_id=device, device_id_type=MESH)
         return carry
 
+    lax.fori_loop(1, devices, greet, 0)
     inputs = [
         pltpu.make_async_copy(src, dst, trace_sem.at[at])
         for at, (src, dst) in enumerate(
@@ -200,7 +215,6 @@
     ]
     for load in inputs:
         load.start()
-    lax.fori_loop(1, devices, greet, 0)
     loads = [
         pltpu.make_async_copy(src, dst, table_sem.at[at])
         for at, (src, dst) in enumerate(
@@ -210,6 +224,7 @@
                 (modes_x_hbm, modes_x),
                 (modes_y_hbm, modes_y),
                 (hart_hbm, hart),
+                (slow_hbm, slow_ref),
             ]
         )
     ]
@@ -297,6 +312,8 @@
     arrive, leave_route = spread(route_out, route_in, route_sent, route_got)
     route_in[pl.ds(me, 1)] = route_out[pl.ds(me, 1)]
 
+    for load in loads:
+        load.wait()
     frequency = freq_ref[0]
     waves = []
     for depth_at in range(2):
@@ -309,21 +326,34 @@
             squares.append((reference, (frequency * reference) * (frequency * reference)))
         waves.append(squares)
 
-    chunk = 8
+    chunk = 16
+    quarter_x, quarter_y = nx // 4, ny // 4
+    lane = iota((chunk, quarter_y), 1)
+    first_ky = [wave_number(lane + parity * half_y, ny) for parity in range(2)]
+    middle_ky = jnp.full((chunk, quarter_y), math.pi, jnp.float32)
+
+    def wide_rows(g, kx):
+        made = [propagator(waves[0][g][1], kx, ky) for ky in (*first_ky, middle_ky)]
+        return [
+            jnp.concatenate([even, jnp.where(lane == 0, middle, even), odd, odd], 1)
+            for even, odd, middle in zip(*made)
+        ]
 
     def wide_tables(at, carry):
-        first = pl.multiple_of(at * chunk, chunk)
-        kx = signed(iota((chunk, ny), 0) + first, nx)
-        ky = signed(iota((chunk, ny), 1), ny)
+        first = pl.multiple_of(lax.rem(at, quarter_x // chunk) * chunk, chunk)
+        base = pl.multiple_of(lax.div(at, quarter_x // chunk) * half_x, half_x)
+        kx = wave_number(iota((chunk, quarter_y), 0) + (first + base), nx)
         for g in range(REFS):
-            even, odd = propagator(waves[0][g][1], kx, ky)
-            wide_even[g, pl.ds(first, chunk), :] = even
-            wide_odd[g, pl.ds(first, chunk), :] = odd
+            for one, table in zip(wide_rows(g, kx), (wide_even, wide_odd)):
+                for copy in range(2):
+                    table[g, pl.ds(base + copy * quarter_x + first, chunk), :] = one
         return carry
 
-    lax.fori_loop(0, nx // chunk, wide_tables, 0)
-    for load in loads:
-        load.wait()
+    lax.fori_loop(0, half_x // chunk, wide_tables, 0)
+    middle_kx = jnp.full((chunk, quarter_y), math.pi, jnp.float32)
+    for g in range(REFS):
+        for one, table in zip(wide_rows(g, middle_kx), (wide_even, wide_odd)):
+            table[g, quarter_x : quarter_x + 1, :] = one[:1]
     arrive()
 
     mirror = pltpu.make_async_remote_copy(
@@ -337,7 +367,7 @@
     mirror.start()
 
     group_at = lax.div(lax.rem(iota((data_rows, 2 * slots), 1), slots), CAP)
-    eye = jnp.where(iota((TERMS, TERMS + data_rows), 0) == iota((TERMS, TERMS + data_rows), 1), damping, 0.0)
+    eye = jnp.where(iota((TERMS + data_rows, TERMS), 0) == iota((TERMS + data_rows, TERMS), 1), damping, 0.0)
 
     def chebyshev(cosine):
         terms = [jnp.ones_like(cosine), cosine]
@@ -345,6 +375,7 @@
             terms.append(2.0 * cosine * terms[-1] - terms[-2])
         return terms
 
+    normals = []
     for t in range(tiles):
         pieces = []
         for first in range(0, devices, tiles):
@@ -359,39 +390,70 @@
         along_y = jnp.concatenate(chebyshev(place[2:3]), 0)
         basis = jnp.concatenate([(term * scale) * along_y for term in along_x], 0)
         right = jnp.concatenate([basis, data], 0)
-        system[t] = eye + lax.dot_general(
-            basis, right, NT, preferred_element_type=jnp.float32, precision=lax.Precision.HIGHEST
+        normals.append(
+            eye
+            + lax.dot_general(
+                right, basis, NT, preferred_element_type=jnp.float32, precision=lax.Precision.HIGHEST
+            )
         )
-    for k in range(TERMS):
-        row = system[:, k : k + 1, :]
-        scaled = row * (1.0 / row[:, :, k : k + 1])
-        whole = system[...]
-        system[...] = whole - whole[:, :, k : k + 1] * scaled
-        system[:, k : k + 1, :] = scaled
-    solved = [jnp.transpose(system[t])[TERMS:] for t in range(tiles)]
+    inner = 128 // tiles
+    outer = TERMS // inner
+    lines = (TERMS + data_rows) // 8
+    rest = []
+    for at in range(outer):
+        line = jnp.concatenate([one[:, at * inner : (at + 1) * inner] for one in normals], 1)
+        rest.append([line[8 * j : 8 * (j + 1)] for j in range(lines)])
+    lane = iota((8, 128), 1)
+    within = lax.rem(lane, inner)
+    for block in range(TERMS // 8):
+        todo = range(block, lines)
+        pivots = []
+        for s in range(8):
+            at, own = (8 * block + s) // inner, (8 * block + s) % inner
+            pick = lane - within + own
+            pivots.append({j: take_lanes(rest[at][j], pick) for j in todo})
+        for s in range(8):
+            at, own = (8 * block + s) // inner, (8 * block + s) % inner
+            scale = 1.0 / pivots[s][block][s : s + 1]
+            scaled = {j: pivots[s][j] * scale for j in todo}
+            for later in range(s + 1, 8):
+                factor = pivots[later][block][s : s + 1]
+                pivots[later] = {j: pivots[later][j] - factor * scaled[j] for j in todo}
+            for one in range(outer):
+                factor = rest[one][block][s : s + 1]
+                for j in todo:
+                    value = rest[one][j] - factor * scaled[j]
+                    rest[one][j] = jnp.where(within == own, scaled[j], value) if one == at else value
     width = tiles * MODES
-    for a in range(MODES):
-        line = jnp.concatenate([one[:, a * MODES : (a + 1) * MODES] for one in solved], 1)
-        for part in range(2):
-            for f in range(F):
-                at = part * F + f
-                coef_out[f, a : a + 1, part * width : (part + 1) * width] = line[at : at + 1]
+    place = lax.rem(lane, width)
+    pick = lax.div(place, MODES) * inner + lax.div(lane, width) * MODES + lax.rem(place, MODES)
+    for one in range(outer):
+        for j in range(TERMS // 8, lines):
+            line = take_lanes(rest[one][j], pick)
+            for s in range(8):
+                part, f = divmod(8 * (j - TERMS // 8) + s, F)
+                coef_out[f, part * outer + one : part * outer + one + 1, :] = line[s : s + 1]
 
     arrive, leave_coef = spread(coef_out, coef_in, coef_sent, coef_got)
     coef_in[pl.ds(me, 1)] = coef_out[pl.ds(me_f, 1)]
 
-    ky = signed(seat * band + iota((chunk, band), 1), ny)
+    band_ky = wave_number(seat * band + iota((chunk, band), 1), ny)
 
     def band_tables(at, carry):
-        first = pl.multiple_of(at * chunk, chunk)
-        kx = signed(iota((chunk, band), 0) + first, nx)
+        first = pl.multiple_of(lax.rem(at, quarter_x // chunk) * chunk, chunk)
+        base = pl.multiple_of(lax.div(at, quarter_x // chunk) * half_x, half_x)
+        kx = wave_number(iota((chunk, band), 0) + (first + base), nx)
         for g in range(REFS):
-            even, odd = propagator(waves[1][g][1], kx, ky)
-            band_even[g, pl.ds(first, chunk), :] = even
-            band_odd[g, pl.ds(first, chunk), :] = odd
+            for one, table in zip(propagator(waves[1][g][1], kx, band_ky), (band_even, band_odd)):
+                for copy in range(2):
+                    table[g, pl.ds(base + copy * quarter_x + first, chunk), :] = one
         return carry
 
-    lax.fori_loop(0, nx // chunk, band_tables, 0)
+    lax.fori_loop(0, half_x // chunk, band_tables, 0)
+    for g in range(REFS):
+        middle = propagator(waves[1][g][1], jnp.full((chunk, band), math.pi, jnp.float32), band_ky)
+        for one, table in zip(middle, (band_even, band_odd)):
+            table[g, quarter_x : quarter_x + 1, :] = one[:1]
 
     def split_step(depth_at, velocity):
         cosine = jnp.zeros(velocity.shape, jnp.float32)
@@ -415,7 +477,7 @@
     def part_of(which):
         return hart[which, 0], hart[which, 1]
 
-    even_k, odd_k, odd_k_t = part_of(0), part_of(1), part_of(2)
+    even_k, even_k_t, odd_k, odd_k_t = (part_of(which) for which in range(4))
 
     def from_modes_of(parts):
         return jnp.concatenate([parts[0], parts[1], parts[0]], 1)
@@ -429,7 +491,17 @@
         lines = [
             jnp.concatenate(
                 [
-                    coef_in[tile_row * per_row + j, :, part * width : (part + 1) * width]
+                    jnp.concatenate(
+                        [
+                            coef_in[
+                                tile_row * per_row + j,
+                                part * outer : (part + 1) * outer,
+                                a * width : (a + 1) * width,
+                            ]
+                            for a in range(MODES // outer)
+                        ],
+                        0,
+                    )
                     for j in range(per_row)
                 ],
                 1,
@@ -457,7 +529,7 @@
         high, low = split2(jnp.concatenate(picked, 1))
         spectrum = dot(modes_x[parity], jnp.concatenate([high, high, low], 0))
         real, imag = spectrum[:, :ny], spectrum[:, ny:]
-        which = 0 if parity == 0 else 2
+        which = 2 * parity + 1
         own_high, own_low = hart[which, 0, seat_rows, :], hart[which, 1, seat_rows, :]
         both = jnp.concatenate([own_high, own_low], 0)
         part = slice(parity * half_x, (parity + 1) * half_x)
@@ -539,7 +611,7 @@
     for p, one in enumerate((real, imag)):
         left, right = one[:, :half_y], one[:, half_y:]
         line = jnp.concatenate(
-            [dot3(split2(left + right), even_k), dot3(split2(left - right), odd_k_t)], 1
+            [dot3(split2(left + right), even_k_t), dot3(split2(left - right), odd_k_t)], 1
         )
         for dst in range(group):
             fwd_out[p, dst] = line[:, dst * band : (dst + 1) * band].reshape(2, rows, band)
@@ -562,7 +634,7 @@
     backward = []
     for g in range(REFS):
         sides = []
-        for parity, table in enumerate((even_k, odd_k_t)):
+        for parity, table in enumerate((even_k_t, odd_k_t)):
             part = slice(parity * half_x, (parity + 1) * half_x)
             even, odd = band_even[g, part, :], band_odd[g, part, :]
             real, imag = spectrum[0][parity], spectrum[1][parity]
@@ -624,7 +696,8 @@
     cfg = (F, L, tiles, nx, ny, rows, data_rows, padded, nvel)
 
     hart = jnp.asarray(half_tables(nx))
-    modes_x, modes_y = (jnp.asarray(one) for one in mode_tables(nx))
+    outer = TERMS * tiles // 128
+    modes_x, modes_y = (jnp.asarray(one) for one in mode_tables(nx, MODES // outer))
 
     f32, bf16, i32 = jnp.float32, jnp.bfloat16, jnp.int32
     dma = pltpu.SemaphoreType.DMA
@@ -634,7 +707,7 @@
             jax.ShapeDtypeStruct((2, rows, ny), f32),
             jax.ShapeDtypeStruct((2, rows, ny // F), f32),
         ],
-        in_specs=[HBM] * 5 + [SMEM] * 2 + [HBM] * 4,
+        in_specs=[HBM] * 5 + [SMEM] + [HBM] * 5,
         out_specs=[VMEM, VMEM],
         scratch_shapes=[
             pltpu.VMEM(spectra.shape, f32),
@@ -642,6 +715,7 @@
             pltpu.VMEM((1, count), i32),
             pltpu.VMEM((2, count), f32),
             pltpu.VMEM((1, count), f32),
+            pltpu.SMEM(slowness.shape, f32),
             pltpu.VMEM(hart.shape, bf16),
             pltpu.VMEM(modes_x.shape, bf16),
             pltpu.VMEM(modes_y.shape, bf16),
@@ -649,9 +723,8 @@
             pltpu.VMEM((rows, ny), i32),
             pltpu.VMEM((devices, data_rows, 2 * slots), f32),
             pltpu.VMEM((devices, data_rows, 2 * slots), f32),
-            pltpu.VMEM((tiles, TERMS, TERMS + data_rows), f32),
-            pltpu.VMEM((F, MODES, 2 * tiles * MODES), f32),
-            pltpu.VMEM((devices, MODES, 2 * tiles * MODES), f32),
+            pltpu.VMEM((F, 2 * outer, 128), f32),
+            pltpu.VMEM((devices, 2 * outer, 128), f32),
             pltpu.VMEM((REFS, nx, ny), f32),
             pltpu.VMEM((REFS, nx, ny), f32),
             pltpu.VMEM((REFS, nx, band), f32),
@@ -667,7 +740,7 @@
             pltpu.VMEM((2, F, rows, ny // F), f32),
             pltpu.VMEM((2, F, rows, ny // F), f32),
             dma((5,)),
-            dma((5,)),
+            dma((6,)),
             dma((devices,)),
             dma((devices,)),
             dma((devices,)),

time: 52.5 us -> 50 us (0.952)
  Pallas kernels: 49.6 us -> 47.2 us
    pallas_call x1, Pallas kernels: 49.6 us -> 47.2 us  [local(): pl.pallas_call(functools.partial(program, cfg), out_shape=[jax.ShapeDtype...]
where the time goes in v4:
time: 50 us; the launch traced here: 49.8 us
  Pallas kernels  47.2 us (94%)
  local copies, waits for them, and re-layouts  1.33 us (3%)
  between operations  1.29 us (3%)
    pallas_call x1, Pallas kernels, local(): pl.pallas_call(functools.partial(program, cfg), out_shape=[jax.ShapeDtype...  47.2 us
    unnamed x2, local copies, waits for them, and re-layouts  1.33 us

profile of v4, /device:TPU:0, one launch (start us, length us, event | category | flops | bytes accessed | tf_op | source)
XLA Modules:
  0.0 49.8 jit_solution(7239339112741013083)
XLA Ops:
  1.3 47.2 %shard_map.122 = (f32[2,64,512]{2,1,0:T(8,128)S(1)}, f32[2,64,128]{2,1,0:T(8,128)S(1)}) custom-call(f32[2,4,1024]{2,1,0:T(4,128)} %spectra_hbm.1, s32[1,1024]{1,0:T(1,128)} %bitcast.7, s32[1,1024]{1,0:T(1,128)} %bitcast.8, f32[2,1024]{1,0:T(2,128)} %offset_hbm.1, f32[1,1024]{1,0:T(1,128)} %bitcast.9, f32[1]{0:T(128)S(6)} %copy.16.freq_ref, f32[2,8]{1,0:T(2,128)} %slow_hbm.1, ...), custom_call_target="tpu_custom_call" | custom-call | tf_op jit(solution)/shard_map/pallas_call | solution.py:704
  48.5 0.7 %copy.17 = f32[2,1,64,512]{3,2,1,0:T(8,128)} copy(f32[2,1,64,512]{3,2,1,0:T(8,128)S(1)} %bitcast.6) | data formatting | bytes 524288
  49.2 0.6 %copy.18 = f32[2,64,128]{2,1,0:T(8,128)} copy(f32[2,64,128]{2,1,0:T(8,128)S(1)} %get-tuple-element.11) | data formatting | bytes 131072

commit v5 on v4

--- a/solution.py
+++ b/solution.py
@@ -132,7 +132,7 @@
     modes_x_hbm,
     modes_y_hbm,
     wave_ref,
-    image_ref,
+    image_in,
     spectra_ref,
     tile_ref,
     bin_ref,
@@ -156,12 +156,13 @@
     across_first,
     along_last,
     across_last,
+    slabs,
+    first_real,
     fwd_out,
     fwd_in,
     back_out,
     back_in,
     image_out,
-    image_in,
     trace_sem,
     table_sem,
     route_sent,
@@ -200,7 +201,6 @@
         pl.semaphore_signal(barrier, inc=1, device_id=device, device_id_type=MESH)
         return carry
 
-    lax.fori_loop(1, devices, greet, 0)
     inputs = [
         pltpu.make_async_copy(src, dst, trace_sem.at[at])
         for at, (src, dst) in enumerate(
@@ -215,6 +215,7 @@
     ]
     for load in inputs:
         load.start()
+    lax.fori_loop(1, devices, greet, 0)
     loads = [
         pltpu.make_async_copy(src, dst, table_sem.at[at])
         for at, (src, dst) in enumerate(
@@ -312,7 +313,21 @@
     arrive, leave_route = spread(route_out, route_in, route_sent, route_got)
     route_in[pl.ds(me, 1)] = route_out[pl.ds(me, 1)]
 
-    for load in loads:
+    parts = F if rows % (8 * F) == 0 else 1
+    part_rows = rows // parts
+    own_part = pl.ds(pl.multiple_of((me_f if parts > 1 else 0) * part_rows, part_rows), part_rows)
+    loads[0].wait()
+    mirror = pltpu.make_async_remote_copy(
+        src_ref=vel_first.at[side, own_part],
+        dst_ref=vel_first.at[side, own_part],
+        send_sem=vel_sem.at[0],
+        recv_sem=vel_sem.at[1],
+        device_id={"lat": lax.rem(me_l + group, L)},
+        device_id_type=MESH,
+    )
+    mirror.start()
+
+    for load in loads[1:]:
         load.wait()
     frequency = freq_ref[0]
     waves = []
@@ -356,15 +371,22 @@
             table[g, quarter_x : quarter_x + 1, :] = one[:1]
     arrive()
 
-    mirror = pltpu.make_async_remote_copy(
-        src_ref=vel_first.at[side],
-        dst_ref=vel_first.at[side],
-        send_sem=vel_sem.at[0],
-        recv_sem=vel_sem.at[1],
-        device_id={"lat": lax.rem(me_l + group, L)},
-        device_id_type=MESH,
-    )
-    mirror.start()
+    mirror.wait_recv()
+    handed = []
+    for step in range(1, parts):
+        other = lax.rem(me_f + step, F)
+        handed.append(
+            pltpu.make_async_remote_copy(
+                src_ref=vel_first.at[1 - side, own_part],
+                dst_ref=vel_first.at[1 - side, own_part],
+                send_sem=vel_sem.at[2 * step],
+                recv_sem=vel_sem.at[2 * step + 1],
+                device_id={"freq": other},
+                device_id_type=MESH,
+            )
+        )
+    for copy in handed:
+        copy.start()
 
     group_at = lax.div(lax.rem(iota((data_rows, 2 * slots), 1), slots), CAP)
     eye = jnp.where(iota((TERMS + data_rows, TERMS), 0) == iota((TERMS + data_rows, TERMS), 1), damping, 0.0)
@@ -469,7 +491,8 @@
         return cosine, sine
 
     along_last[...], across_last[...] = split_step(1, vel_last[...])
-    mirror.wait_recv()
+    for copy in handed:
+        copy.wait_recv()
     for one in range(2):
         along_first[one], across_first[one] = split_step(0, vel_first[one])
     arrive()
@@ -538,11 +561,11 @@
             moved = split2(jnp.concatenate([real * even - imag * odd, real * odd + imag * even], 1))
             back = dot(both, moved[0])
             made[g][parity] = back[:rows] + (back[rows:] + dot(own_high, moved[1]))
-    pieces = []
     for g in range(REFS):
-        slabs = (made[g][0] + made[g][1], made[g][0] - made[g][1])
         for p in range(2):
-            pieces += [slab[:, p * ny : (p + 1) * ny] for slab in slabs]
+            part = slice(p * ny, (p + 1) * ny)
+            for at, slab in enumerate((made[g][0] + made[g][1], made[g][0] - made[g][1])):
+                slabs[at, 2 * g + p] = slab[:, part]
 
     def inverse_y(x):
         u = dot3(split2(x[:, :half_y]), even_k)
@@ -580,7 +603,7 @@
         image_in[depth_at, pl.ds(me_f, 1)] = image_out[depth_at, pl.ds(me_f, 1)]
         return copies
 
-    def exchange(at, out, into, sent, landed):
+    def copies_of(at, out, into, sent, landed):
         copies = []
         for step in range(1, group):
             other = lax.rem(seat + step, group)
@@ -594,36 +617,45 @@
                     device_id_type=MESH,
                 )
             )
+        return copies
+
+    def exchange(at, out, into, sent, landed):
+        copies = copies_of(at, out, into, sent, landed)
         for copy in copies:
             copy.start()
         into[at, pl.ds(seat, 1)] = out[at, pl.ds(seat, 1)]
         return copies
 
-    field = inverse_y(jnp.concatenate(pieces, 0))
-    two = 2 * rows
-    real, imag = choose(
-        [(field[2 * g * two : (2 * g + 1) * two], field[(2 * g + 1) * two : (2 * g + 2) * two]) for g in range(REFS)],
-        vel_first[...].reshape(two, ny),
-    )
-    cosine, sine = along_first[...].reshape(two, ny), across_first[...].reshape(two, ny)
-    real, imag = real * cosine - imag * sine, real * sine + imag * cosine
-    forward = []
-    for p, one in enumerate((real, imag)):
-        left, right = one[:, :half_y], one[:, half_y:]
+    def first_rows(at, carry):
+        field = inverse_y(slabs[at].reshape(2 * REFS * rows, ny))
+        made = [
+            (field[2 * g * rows : (2 * g + 1) * rows], field[(2 * g + 1) * rows : (2 * g + 2) * rows])
+            for g in range(REFS)
+        ]
+        real, imag = choose(made, vel_first[at])
+        cosine, sine = along_first[at], across_first[at]
+        real, imag = real * cosine - imag * sine, real * sine + imag * cosine
+        first_real[at] = real
+        both = jnp.concatenate([real, imag], 0)
+        left, right = both[:, :half_y], both[:, half_y:]
         line = jnp.concatenate(
             [dot3(split2(left + right), even_k_t), dot3(split2(left - right), odd_k_t)], 1
         )
         for dst in range(group):
-            fwd_out[p, dst] = line[:, dst * band : (dst + 1) * band].reshape(2, rows, band)
-        forward.append(exchange(p, fwd_out, fwd_in, fwd_sent, fwd_got))
-    first_image = send_image(0, jnp.where(side == 0, real[:rows], real[rows:]))
+            fwd_out[at, dst] = line[:, dst * band : (dst + 1) * band].reshape(2, rows, band)
+        exchange(at, fwd_out, fwd_in, fwd_sent, fwd_got)
+        return carry
+
+    lax.fori_loop(0, 2, first_rows, 0)
+    forward = [copies_of(at, fwd_out, fwd_in, fwd_sent, fwd_got) for at in range(2)]
+    first_image = send_image(0, first_real[pl.ds(side, 1)].reshape(rows, ny))
 
     spectrum = []
+    for copy in forward[0] + forward[1]:
+        copy.wait_recv()
     for p in range(2):
-        for copy in forward[p]:
-            copy.wait_recv()
-        upper = jnp.concatenate([fwd_in[p, src, 0] for src in range(group)], 0)
-        lower = jnp.concatenate([fwd_in[p, src, 1] for src in range(group)], 0)
+        upper = jnp.concatenate([fwd_in[0, src, p] for src in range(group)], 0)
+        lower = jnp.concatenate([fwd_in[1, src, p] for src in range(group)], 0)
         lines = []
         for one, table in ((upper + lower, even_k), (upper - lower, odd_k)):
             high, low = split2(one)
@@ -662,16 +694,26 @@
     leave_route()
     leave_coef()
     mirror.wait_send()
+    for copy in handed:
+        copy.wait_send()
     for copies in forward + backward:
         for copy in copies:
             copy.wait_send()
-    for depth_at, copies in enumerate((first_image, last_image)):
-        for copy in copies:
-            copy.wait()
-        total = image_in[depth_at, 0]
-        for f in range(1, F):
-            total = total + image_in[depth_at, f]
-        image_ref[depth_at] = total
+    for copy in first_image + last_image:
+        copy.wait()
+
+
+def finish(wave_ref, part_ref, wave_hbm, image_hbm, total, sem):
+    store = pltpu.make_async_copy(wave_ref, wave_hbm.at[:, 0], sem.at[0])
+    store.start()
+    image = part_ref[:, 0]
+    for f in range(1, part_ref.shape[1]):
+        image = image + part_ref[:, f]
+    total[...] = image
+    last = pltpu.make_async_copy(total, image_hbm, sem.at[1])
+    last.start()
+    store.wait()
+    last.wait()
 
 
 def stay(x):
@@ -701,11 +743,11 @@
 
     f32, bf16, i32 = jnp.float32, jnp.bfloat16, jnp.int32
     dma = pltpu.SemaphoreType.DMA
-    wave, image = pl.pallas_call(
+    wave, images = pl.pallas_call(
         functools.partial(program, cfg),
         out_shape=[
             jax.ShapeDtypeStruct((2, rows, ny), f32),
-            jax.ShapeDtypeStruct((2, rows, ny // F), f32),
+            jax.ShapeDtypeStruct((2, F, rows, ny // F), f32),
         ],
         in_specs=[HBM] * 5 + [SMEM] + [HBM] * 5,
         out_specs=[VMEM, VMEM],
@@ -733,11 +775,12 @@
             pltpu.VMEM((2, rows, ny), f32),
             pltpu.VMEM((rows, ny), f32),
             pltpu.VMEM((rows, ny), f32),
+            pltpu.VMEM((2, 2 * REFS, rows, ny), f32),
+            pltpu.VMEM((2, rows, ny), f32),
             pltpu.VMEM((2, group, 2, rows, band), f32),
             pltpu.VMEM((2, group, 2, rows, band), f32),
             pltpu.VMEM((REFS, group, rows, 2 * band), f32),
             pltpu.VMEM((REFS, group, rows, 2 * band), f32),
-            pltpu.VMEM((2, F, rows, ny // F), f32),
             pltpu.VMEM((2, F, rows, ny // F), f32),
             dma((5,)),
             dma((6,)),
@@ -745,7 +788,7 @@
             dma((devices,)),
             dma((devices,)),
             dma((devices,)),
-            dma((2,)),
+            dma((2 * F,)),
             dma((2, group)),
             dma((2, group)),
             dma((REFS, group)),
@@ -763,7 +806,17 @@
         stay(slowness),
         *map(stay, (vel_index, hart, modes_x, modes_y)),
     )
-    return wave[:, None], image
+    return pl.pallas_call(
+        finish,
+        out_shape=[
+            jax.ShapeDtypeStruct((2, 1, rows, ny), f32),
+            jax.ShapeDtypeStruct((2, rows, ny // F), f32),
+        ],
+        in_specs=[VMEM, VMEM],
+        out_specs=[HBM, HBM],
+        scratch_shapes=[pltpu.VMEM((2, rows, ny // F), f32), dma((2,))],
+        compiler_params=pltpu.CompilerParams(vmem_limit_bytes=8 << 20),
+    )(wave, images)
 
 
 def solution(mesh):

time: 50 us -> 47.2 us (0.944)
  Pallas kernels: 47.2 us -> 45.7 us
  local copies, waits for them, and re-layouts: 1.33 us -> 0 us
    pallas_call x1, Pallas kernels: 47.2 us -> 44.9 us  [local(): pl.pallas_call(functools.partial(program, cfg), out_shape=[jax.ShapeDtype...]
    unnamed x2 -> x0, local copies, waits for them, and re-layouts: 1.33 us -> none
    pallas_call x0 -> x1, Pallas kernels: none -> 0.74 us  [local(): pl.pallas_call(finish, out_shape=[jax.ShapeDtypeStruct((2, 1, rows, ny),...]
where the time goes in v5:
time: 47.2 us; the launch traced here: 47 us
  Pallas kernels  45.7 us (97%)
  between operations  1.29 us (3%)
    pallas_call x1, Pallas kernels, local(): pl.pallas_call(functools.partial(program, cfg), out_shape=[jax.ShapeDtype...  44.9 us

profile of v5, /device:TPU:0, one launch (start us, length us, event | category | flops | bytes accessed | tf_op | source)
XLA Modules:
  0.0 47.0 jit_solution(6345865665368962631)
XLA Ops:
  1.3 44.9 %shard_map.122 = (f32[2,64,512]{2,1,0:T(8,128)S(1)}, f32[2,4,64,128]{3,2,1,0:T(8,128)S(1)}) custom-call(f32[2,4,1024]{2,1,0:T(4,128)} %spectra_hbm.1, s32[1,1024]{1,0:T(1,128)} %bitcast.3, s32[1,1024]{1,0:T(1,128)} %bitcast.4, f32[2,1024]{1,0:T(2,128)} %offset_hbm.1, f32[1,1024]{1,0:T(1,128)} %bitcast.5, f32[1]{0:T(128)S(6)} %copy.13.freq_ref, ...), custom_call_target="tpu_custom_call" | custom-call | tf_op jit(solution)/shard_map/pallas_call | solution.py:746
  46.2 0.7 %shard_map.123 = (f32[2,1,64,512]{3,2,1,0:T(8,128)}, f32[2,64,128]{2,1,0:T(8,128)}) custom-call(f32[2,64,512]{2,1,0:T(8,128)S(1)} %get-tuple-element.4.wave_ref, f32[2,4,64,128]{3,2,1,0:T(8,128)S(1)} %get-tuple-element.5.part_ref), custom_call_target="tpu_custom_call" | custom-call | tf_op jit(solution)/shard_map/pallas_call | solution.py:809

commit v6 on v5

--- a/solution.py
+++ b/solution.py
@@ -268,6 +268,7 @@
     middle = rest.astype(jnp.bfloat16)
     low = (rest - middle.astype(jnp.float32)).astype(jnp.bfloat16)
     parts = jnp.concatenate([high, middle, low], 0)
+    fold = (data_rows + 4) // 2
     wide = 256
     for at in range(0, devices * slots, wide):
         places = iota((wide, count), 0) + at
@@ -276,7 +277,7 @@
         got = got[:padded] + got[padded : 2 * padded] + got[2 * padded :]
         for piece in range(wide // slots):
             block = got[:, piece * slots : (piece + 1) * slots]
-            route_out[at // slots + piece] = jnp.concatenate([block[:data_rows], block[data_rows:]], 1)
+            route_out[at // slots + piece] = jnp.concatenate([block[:fold], block[fold : 2 * fold]], 1)
 
     pl.semaphore_wait(barrier, devices - 1)
 
@@ -313,21 +314,7 @@
     arrive, leave_route = spread(route_out, route_in, route_sent, route_got)
     route_in[pl.ds(me, 1)] = route_out[pl.ds(me, 1)]
 
-    parts = F if rows % (8 * F) == 0 else 1
-    part_rows = rows // parts
-    own_part = pl.ds(pl.multiple_of((me_f if parts > 1 else 0) * part_rows, part_rows), part_rows)
-    loads[0].wait()
-    mirror = pltpu.make_async_remote_copy(
-        src_ref=vel_first.at[side, own_part],
-        dst_ref=vel_first.at[side, own_part],
-        send_sem=vel_sem.at[0],
-        recv_sem=vel_sem.at[1],
-        device_id={"lat": lax.rem(me_l + group, L)},
-        device_id_type=MESH,
-    )
-    mirror.start()
-
-    for load in loads[1:]:
+    for load in loads:
         load.wait()
     frequency = freq_ref[0]
     waves = []
@@ -371,24 +358,20 @@
             table[g, quarter_x : quarter_x + 1, :] = one[:1]
     arrive()
 
-    mirror.wait_recv()
-    handed = []
-    for step in range(1, parts):
-        other = lax.rem(me_f + step, F)
-        handed.append(
-            pltpu.make_async_remote_copy(
-                src_ref=vel_first.at[1 - side, own_part],
-                dst_ref=vel_first.at[1 - side, own_part],
-                send_sem=vel_sem.at[2 * step],
-                recv_sem=vel_sem.at[2 * step + 1],
-                device_id={"freq": other},
-                device_id_type=MESH,
-            )
-        )
-    for copy in handed:
-        copy.start()
-
-    group_at = lax.div(lax.rem(iota((data_rows, 2 * slots), 1), slots), CAP)
+    parts = F if rows % (8 * F) == 0 else 1
+    part_rows = rows // parts
+    own_part = pl.ds(pl.multiple_of((me_f if parts > 1 else 0) * part_rows, part_rows), part_rows)
+    mirror = pltpu.make_async_remote_copy(
+        src_ref=vel_first.at[side, own_part],
+        dst_ref=vel_first.at[side, own_part],
+        send_sem=vel_sem.at[0],
+        recv_sem=vel_sem.at[1],
+        device_id={"lat": lax.rem(me_l + group, L)},
+        device_id_type=MESH,
+    )
+    mirror.start()
+
+    group_at = lax.div(lax.rem(iota((fold, 2 * slots), 1), slots), CAP)
     eye = jnp.where(iota((TERMS + data_rows, TERMS), 0) == iota((TERMS + data_rows, TERMS), 1), damping, 0.0)
 
     def chebyshev(cosine):
@@ -406,7 +389,9 @@
                 picked = jnp.where(group_at == (t + i) % tiles, route_in[first + i], picked)
             pieces.append(picked)
         data = jnp.concatenate([piece[:, :slots] for piece in pieces], 1)
-        place = jnp.concatenate([piece[:8, slots:] for piece in pieces], 1)
+        place = jnp.concatenate([piece[:, slots:] for piece in pieces], 1)
+        data = jnp.concatenate([data, place[: data_rows - fold]], 0)
+        place = place[data_rows - fold :]
         scale = place[0:1]
         along_x = chebyshev(place[1:2])
         along_y = jnp.concatenate(chebyshev(place[2:3]), 0)
@@ -458,6 +443,23 @@
 
     arrive, leave_coef = spread(coef_out, coef_in, coef_sent, coef_got)
     coef_in[pl.ds(me, 1)] = coef_out[pl.ds(me_f, 1)]
+
+    mirror.wait_recv()
+    handed = []
+    for step in range(1, parts):
+        other = lax.rem(me_f + step, F)
+        handed.append(
+            pltpu.make_async_remote_copy(
+                src_ref=vel_first.at[1 - side, own_part],
+                dst_ref=vel_first.at[1 - side, own_part],
+                send_sem=vel_sem.at[2 * step],
+                recv_sem=vel_sem.at[2 * step + 1],
+                device_id={"freq": other},
+                device_id_type=MESH,
+            )
+        )
+    for copy in handed:
+        copy.start()
 
     band_ky = wave_number(seat * band + iota((chunk, band), 1), ny)
 
@@ -763,8 +765,8 @@
             pltpu.VMEM(modes_y.shape, bf16),
             pltpu.VMEM((2, rows, ny), i32),
             pltpu.VMEM((rows, ny), i32),
-            pltpu.VMEM((devices, data_rows, 2 * slots), f32),
-            pltpu.VMEM((devices, data_rows, 2 * slots), f32),
+            pltpu.VMEM((devices, (data_rows + 4) // 2, 2 * slots), f32),
+            pltpu.VMEM((devices, (data_rows + 4) // 2, 2 * slots), f32),
             pltpu.VMEM((F, 2 * outer, 128), f32),
             pltpu.VMEM((devices, 2 * outer, 128), f32),
             pltpu.VMEM((REFS, nx, ny), f32),

time: 47.2 us -> 45.8 us (0.970)
  Pallas kernels: 45.7 us -> 44.3 us
    pallas_call x1, Pallas kernels: 44.9 us -> 43.6 us  [local(): pl.pallas_call(functools.partial(program, cfg), out_shape=[jax.ShapeDtype...]
where the time goes in v6:
time: 45.8 us; the launch traced here: 45.6 us
  Pallas kernels  44.3 us (97%)
  between operations  1.29 us (3%)
    pallas_call x1, Pallas kernels, local(): pl.pallas_call(functools.partial(program, cfg), out_shape=[jax.ShapeDtype...  43.6 us

profile of v6, /device:TPU:0, one launch (start us, length us, event | category | flops | bytes accessed | tf_op | source)
XLA Modules:
  0.0 45.6 jit_solution(9751353022644342327)
XLA Ops:
  1.3 43.6 %shard_map.122 = (f32[2,64,512]{2,1,0:T(8,128)S(1)}, f32[2,4,64,128]{3,2,1,0:T(8,128)S(1)}) custom-call(f32[2,4,1024]{2,1,0:T(4,128)} %spectra_hbm.1, s32[1,1024]{1,0:T(1,128)} %bitcast.3, s32[1,1024]{1,0:T(1,128)} %bitcast.4, f32[2,1024]{1,0:T(2,128)} %offset_hbm.1, f32[1,1024]{1,0:T(1,128)} %bitcast.5, f32[1]{0:T(128)S(6)} %copy.13.freq_ref, ...), custom_call_target="tpu_custom_call" | custom-call | tf_op jit(solution)/shard_map/pallas_call | solution.py:748
  44.9 0.7 %shard_map.123 = (f32[2,1,64,512]{3,2,1,0:T(8,128)}, f32[2,64,128]{2,1,0:T(8,128)}) custom-call(f32[2,64,512]{2,1,0:T(8,128)S(1)} %get-tuple-element.4.wave_ref, f32[2,4,64,128]{3,2,1,0:T(8,128)S(1)} %get-tuple-element.5.part_ref), custom_call_target="tpu_custom_call" | custom-call | tf_op jit(solution)/shard_map/pallas_call | solution.py:811

commit v7 on v6

--- a/solution.py
+++ b/solution.py
@@ -14,6 +14,7 @@
 CAP = 8
 TERMS = MODES * MODES
 REFS = 2
+CHUNKS = 2
 
 damping = 1.0
 depth_step = 1.0
@@ -182,6 +183,8 @@
     group = L // 2
     half_x, half_y = nx // 2, ny // 2
     band = ny // group
+    span = band // CHUNKS
+    pair = 2 * span
     slots = tiles * CAP
     per_group = nvel // REFS
     me_f = lax.axis_index("freq")
@@ -461,23 +464,32 @@
     for copy in handed:
         copy.start()
 
-    band_ky = wave_number(seat * band + iota((chunk, band), 1), ny)
+    pair_lane = iota((chunk, pair), 1)
+    sign = jnp.where(pair_lane < span, -1.0, 1.0)
+    band_ky = [
+        wave_number(seat * band + c * span + lax.rem(pair_lane, span), ny) for c in range(CHUNKS)
+    ]
+
+    def band_rows(c, g, kx):
+        even, odd = propagator(waves[1][g][1], kx, band_ky[c])
+        return (even, band_even), (odd * sign, band_odd)
 
     def band_tables(at, carry):
         first = pl.multiple_of(lax.rem(at, quarter_x // chunk) * chunk, chunk)
         base = pl.multiple_of(lax.div(at, quarter_x // chunk) * half_x, half_x)
-        kx = wave_number(iota((chunk, band), 0) + (first + base), nx)
+        kx = wave_number(iota((chunk, pair), 0) + (first + base), nx)
+        for c in range(CHUNKS):
+            for g in range(REFS):
+                for one, table in band_rows(c, g, kx):
+                    for copy in range(2):
+                        table[c, g, pl.ds(base + copy * quarter_x + first, chunk), :] = one
+        return carry
+
+    lax.fori_loop(0, half_x // chunk, band_tables, 0)
+    for c in range(CHUNKS):
         for g in range(REFS):
-            for one, table in zip(propagator(waves[1][g][1], kx, band_ky), (band_even, band_odd)):
-                for copy in range(2):
-                    table[g, pl.ds(base + copy * quarter_x + first, chunk), :] = one
-        return carry
-
-    lax.fori_loop(0, half_x // chunk, band_tables, 0)
-    for g in range(REFS):
-        middle = propagator(waves[1][g][1], jnp.full((chunk, band), math.pi, jnp.float32), band_ky)
-        for one, table in zip(middle, (band_even, band_odd)):
-            table[g, quarter_x : quarter_x + 1, :] = one[:1]
+            for one, table in band_rows(c, g, jnp.full((chunk, pair), math.pi, jnp.float32)):
+                table[c, g, quarter_x : quarter_x + 1, :] = one[:1]
 
     def split_step(depth_at, velocity):
         cosine = jnp.zeros(velocity.shape, jnp.float32)
@@ -544,30 +556,40 @@
         for parity, one in enumerate((sums, differences))
     ]
     seat_rows = pl.ds(pl.multiple_of(seat * rows, rows), rows)
-    made = [[None, None] for _ in range(REFS)]
+    spans = []
     for parity in range(2):
-        picked = [
-            one[(2 * p + parity) * mode_rows : (2 * p + parity + 1) * mode_rows]
-            for p in range(2)
-            for one in spread_y
-        ]
-        high, low = split2(jnp.concatenate(picked, 1))
-        spectrum = dot(modes_x[parity], jnp.concatenate([high, high, low], 0))
-        real, imag = spectrum[:, :ny], spectrum[:, ny:]
-        which = 2 * parity + 1
+        parts = []
+        for p in range(2):
+            at = (2 * p + parity) * mode_rows
+            line = jnp.concatenate([one[at : at + mode_rows] for one in spread_y], 1)
+            parts.append(split2(line))
+        spans.append(parts)
+    seats = []
+    for which in (1, 3):
         own_high, own_low = hart[which, 0, seat_rows, :], hart[which, 1, seat_rows, :]
-        both = jnp.concatenate([own_high, own_low], 0)
-        part = slice(parity * half_x, (parity + 1) * half_x)
+        seats.append((own_high, jnp.concatenate([own_high, own_low], 0)))
+    wide = 128
+    for first in range(0, ny, wide):
+        lanes = slice(first, first + wide)
+        made = [[None, None] for _ in range(REFS)]
+        for parity in range(2):
+            high = jnp.concatenate([one[0][:, lanes] for one in spans[parity]], 1)
+            low = jnp.concatenate([one[1][:, lanes] for one in spans[parity]], 1)
+            spectrum = dot(modes_x[parity], jnp.concatenate([high, high, low], 0))
+            real, imag = spectrum[:, :wide], spectrum[:, wide:]
+            own_high, both = seats[parity]
+            part = slice(parity * half_x, (parity + 1) * half_x)
+            for g in range(REFS):
+                even, odd = wide_even[g, part, lanes], wide_odd[g, part, lanes]
+                moved = split2(
+                    jnp.concatenate([real * even - imag * odd, real * odd + imag * even], 1)
+                )
+                back = dot(both, moved[0])
+                made[g][parity] = back[:rows] + (back[rows:] + dot(own_high, moved[1]))
         for g in range(REFS):
-            even, odd = wide_even[g, part, :], wide_odd[g, part, :]
-            moved = split2(jnp.concatenate([real * even - imag * odd, real * odd + imag * even], 1))
-            back = dot(both, moved[0])
-            made[g][parity] = back[:rows] + (back[rows:] + dot(own_high, moved[1]))
-    for g in range(REFS):
-        for p in range(2):
-            part = slice(p * ny, (p + 1) * ny)
             for at, slab in enumerate((made[g][0] + made[g][1], made[g][0] - made[g][1])):
-                slabs[at, 2 * g + p] = slab[:, part]
+                for p in range(2):
+                    slabs[at, 2 * g + p, :, lanes] = slab[:, p * wide : (p + 1) * wide]
 
     def inverse_y(x):
         u = dot3(split2(x[:, :half_y]), even_k)
@@ -605,27 +627,27 @@
         image_in[depth_at, pl.ds(me_f, 1)] = image_out[depth_at, pl.ds(me_f, 1)]
         return copies
 
-    def copies_of(at, out, into, sent, landed):
+    def copies_of(at, c, out, into, sent, landed):
         copies = []
         for step in range(1, group):
             other = lax.rem(seat + step, group)
             copies.append(
                 pltpu.make_async_remote_copy(
-                    src_ref=out.at[at, other],
-                    dst_ref=into.at[at, seat],
-                    send_sem=sent.at[at, step],
-                    recv_sem=landed.at[at, step],
+                    src_ref=out.at[at, c, other],
+                    dst_ref=into.at[at, c, seat],
+                    send_sem=sent.at[at, c, step],
+                    recv_sem=landed.at[at, c, step],
                     device_id={"lat": side * group + other},
                     device_id_type=MESH,
                 )
             )
         return copies
 
-    def exchange(at, out, into, sent, landed):
-        copies = copies_of(at, out, into, sent, landed)
+    def exchange(at, c, out, into, sent, landed):
+        copies = copies_of(at, c, out, into, sent, landed)
         for copy in copies:
             copy.start()
-        into[at, pl.ds(seat, 1)] = out[at, pl.ds(seat, 1)]
+        into[at, c, pl.ds(seat, 1)] = out[at, c, pl.ds(seat, 1)]
         return copies
 
     def first_rows(at, carry):
@@ -643,45 +665,60 @@
         line = jnp.concatenate(
             [dot3(split2(left + right), even_k_t), dot3(split2(left - right), odd_k_t)], 1
         )
-        for dst in range(group):
-            fwd_out[at, dst] = line[:, dst * band : (dst + 1) * band].reshape(2, rows, band)
-        exchange(at, fwd_out, fwd_in, fwd_sent, fwd_got)
+        for c in range(CHUNKS):
+            for dst in range(group):
+                part = slice(dst * band + c * span, dst * band + (c + 1) * span)
+                fwd_out[at, c, dst] = jnp.concatenate([line[:rows, part], line[rows:, part]], 1)
+        exchange(at, 0, fwd_out, fwd_in, fwd_sent, fwd_got)
         return carry
 
     lax.fori_loop(0, 2, first_rows, 0)
-    forward = [copies_of(at, fwd_out, fwd_in, fwd_sent, fwd_got) for at in range(2)]
+    forward = [[copies_of(at, 0, fwd_out, fwd_in, fwd_sent, fwd_got) for at in range(2)]]
+    for c in range(1, CHUNKS):
+        forward.append([exchange(at, c, fwd_out, fwd_in, fwd_sent, fwd_got) for at in range(2)])
+    forward = [sum(copies, []) for copies in forward]
     first_image = send_image(0, first_real[pl.ds(side, 1)].reshape(rows, ny))
 
-    spectrum = []
-    for copy in forward[0] + forward[1]:
-        copy.wait_recv()
-    for p in range(2):
-        upper = jnp.concatenate([fwd_in[0, src, p] for src in range(group)], 0)
-        lower = jnp.concatenate([fwd_in[1, src, p] for src in range(group)], 0)
-        lines = []
+    turn = (1 - 2 * side).astype(jnp.float32)
+
+    def apply(table, x):
+        high, low = split2(x)
+        made = dot(table[0], jnp.concatenate([high, low], 1))
+        return made[:, :pair] + (made[:, pair:] + dot(table[1], high))
+
+    backward = []
+    for c in range(CHUNKS):
+        for copy in forward[c]:
+            copy.wait_recv()
+        upper, lower = fwd_in[0, c].reshape(half_x, pair), fwd_in[1, c].reshape(half_x, pair)
+        spectrum = []
         for one, table in ((upper + lower, even_k), (upper - lower, odd_k)):
-            high, low = split2(one)
-            line = dot(table[0], jnp.concatenate([high, low], 1))
-            lines.append(line[:, :band] + (line[:, band:] + dot(table[1], high)))
-        spectrum.append(lines)
-    turn = (1 - 2 * side).astype(jnp.float32)
-    backward = []
-    for g in range(REFS):
-        sides = []
-        for parity, table in enumerate((even_k_t, odd_k_t)):
-            part = slice(parity * half_x, (parity + 1) * half_x)
-            even, odd = band_even[g, part, :], band_odd[g, part, :]
-            real, imag = spectrum[0][parity], spectrum[1][parity]
-            moved = jnp.concatenate([real * even - imag * odd, real * odd + imag * even], 1)
-            sides.append(dot3(table, split2(moved)))
-        back_out[g] = (sides[0] + turn * sides[1]).reshape(group, rows, 2 * band)
-        backward.append(exchange(g, back_out, back_in, back_sent, back_got))
+            line = apply(table, one)
+            spectrum.append((line, jnp.concatenate([line[:, span:], line[:, :span]], 1)))
+        for g in range(REFS):
+            sides = []
+            for parity, table in enumerate((even_k_t, odd_k_t)):
+                part = slice(parity * half_x, (parity + 1) * half_x)
+                line, swapped = spectrum[parity]
+                sides.append(
+                    apply(table, line * band_even[c, g, part, :] + swapped * band_odd[c, g, part, :])
+                )
+            back_out[g, c] = (sides[0] + turn * sides[1]).reshape(group, rows, pair)
+            backward.append(exchange(g, c, back_out, back_in, back_sent, back_got))
     made = []
     for g in range(REFS):
-        for copy in backward[g]:
-            copy.wait_recv()
+        for c in range(CHUNKS):
+            for copy in backward[c * REFS + g]:
+                copy.wait_recv()
         lines = [
-            jnp.concatenate([back_in[g, src, :, p * band : (p + 1) * band] for src in range(group)], 1)
+            jnp.concatenate(
+                [
+                    back_in[g, c, src, :, p * span : (p + 1) * span]
+                    for src in range(group)
+                    for c in range(CHUNKS)
+                ],
+                1,
+            )
             for p in range(2)
         ]
         field = inverse_y(jnp.concatenate(lines, 0))
@@ -735,7 +772,7 @@
     data_rows = 2 * spectra.shape[1]
     padded = 2 * data_rows
     group = L // 2
-    band = ny // group
+    pair = 2 * (ny // group) // CHUNKS
     nvel = slowness.shape[1]
     cfg = (F, L, tiles, nx, ny, rows, data_rows, padded, nvel)
 
@@ -771,18 +808,18 @@
             pltpu.VMEM((devices, 2 * outer, 128), f32),
             pltpu.VMEM((REFS, nx, ny), f32),
             pltpu.VMEM((REFS, nx, ny), f32),
-            pltpu.VMEM((REFS, nx, band), f32),
-            pltpu.VMEM((REFS, nx, band), f32),
+            pltpu.VMEM((CHUNKS, REFS, nx, pair), f32),
+            pltpu.VMEM((CHUNKS, REFS, nx, pair), f32),
             pltpu.VMEM((2, rows, ny), f32),
             pltpu.VMEM((2, rows, ny), f32),
             pltpu.VMEM((rows, ny), f32),
             pltpu.VMEM((rows, ny), f32),
             pltpu.VMEM((2, 2 * REFS, rows, ny), f32),
             pltpu.VMEM((2, rows, ny), f32),
-            pltpu.VMEM((2, group, 2, rows, band), f32),
-            pltpu.VMEM((2, group, 2, rows, band), f32),
-            pltpu.VMEM((REFS, group, rows, 2 * band), f32),
-            pltpu.VMEM((REFS, group, rows, 2 * band), f32),
+            pltpu.VMEM((2, CHUNKS, group, rows, pair), f32),
+            pltpu.VMEM((2, CHUNKS, group, rows, pair), f32),
+            pltpu.VMEM((REFS, CHUNKS, group, rows, pair), f32),
+            pltpu.VMEM((REFS, CHUNKS, group, rows, pair), f32),
             pltpu.VMEM((2, F, rows, ny // F), f32),
             dma((5,)),
             dma((6,)),
@@ -791,10 +828,10 @@
             dma((devices,)),
             dma((devices,)),
             dma((2 * F,)),
-            dma((2, group)),
-            dma((2, group)),
-            dma((REFS, group)),
-            dma((REFS, group)),
+            dma((2, CHUNKS, group)),
+            dma((2, CHUNKS, group)),
+            dma((REFS, CHUNKS, group)),
+            dma((REFS, CHUNKS, group)),
             dma((2, F)),
             dma((2, F)),
         ],

time: 45.8 us -> 44.2 us (0.965)
  Pallas kernels: 44.3 us -> 42.7 us
    pallas_call x1, Pallas kernels: 43.6 us -> 42 us  [local(): pl.pallas_call(functools.partial(program, cfg), out_shape=[jax.ShapeDtype...]
where the time goes in v7:
time: 44.2 us; the launch traced here: 44 us
  Pallas kernels  42.7 us (97%)
  between operations  1.29 us (3%)
    pallas_call x1, Pallas kernels, local(): pl.pallas_call(functools.partial(program, cfg), out_shape=[jax.ShapeDtype...  42 us

profile of v7, /device:TPU:0, one launch (start us, length us, event | category | flops | bytes accessed | tf_op | source)
XLA Modules:
  0.0 44.0 jit_solution(17842053755271491997)
XLA Ops:
  1.3 42.0 %shard_map.122 = (f32[2,64,512]{2,1,0:T(8,128)S(1)}, f32[2,4,64,128]{3,2,1,0:T(8,128)S(1)}) custom-call(f32[2,4,1024]{2,1,0:T(4,128)} %spectra_hbm.1, s32[1,1024]{1,0:T(1,128)} %bitcast.3, s32[1,1024]{1,0:T(1,128)} %bitcast.4, f32[2,1024]{1,0:T(2,128)} %offset_hbm.1, f32[1,1024]{1,0:T(1,128)} %bitcast.5, f32[1]{0:T(128)S(6)} %copy.13.freq_ref, ...), custom_call_target="tpu_custom_call" | custom-call | tf_op jit(solution)/shard_map/pallas_call | solution.py:785
  43.3 0.7 %shard_map.123 = (f32[2,1,64,512]{3,2,1,0:T(8,128)}, f32[2,64,128]{2,1,0:T(8,128)}) custom-call(f32[2,64,512]{2,1,0:T(8,128)S(1)} %get-tuple-element.4.wave_ref, f32[2,4,64,128]{3,2,1,0:T(8,128)S(1)} %get-tuple-element.5.part_ref), custom_call_target="tpu_custom_call" | custom-call | tf_op jit(solution)/shard_map/pallas_call | solution.py:848

commit v8 on v7

--- a/solution.py
+++ b/solution.py
@@ -606,25 +606,26 @@
 
     image_piece = ny // F
 
-    def send_image(depth_at, real):
+    def send_image(at, depth_at, first, real):
+        part = slice(first, first + real.shape[0])
         for f in range(F):
-            image_out[depth_at, f] = real[:, f * image_piece : (f + 1) * image_piece]
+            image_out[depth_at, f, part, :] = real[:, f * image_piece : (f + 1) * image_piece]
         copies = []
         for step in range(1, F):
             other = lax.rem(me_f + step, F)
             copies.append(
                 pltpu.make_async_remote_copy(
-                    src_ref=image_out.at[depth_at, other],
-                    dst_ref=image_in.at[depth_at, me_f],
-                    send_sem=image_sent.at[depth_at, step],
-                    recv_sem=image_got.at[depth_at, step],
+                    src_ref=image_out.at[depth_at, other, part],
+                    dst_ref=image_in.at[depth_at, me_f, part],
+                    send_sem=image_sent.at[at, step],
+                    recv_sem=image_got.at[at, step],
                     device_id={"freq": other},
                     device_id_type=MESH,
                 )
             )
         for copy in copies:
             copy.start()
-        image_in[depth_at, pl.ds(me_f, 1)] = image_out[depth_at, pl.ds(me_f, 1)]
+        image_in[depth_at, pl.ds(me_f, 1), part, :] = image_out[depth_at, pl.ds(me_f, 1), part, :]
         return copies
 
     def copies_of(at, c, out, into, sent, landed):
@@ -677,9 +678,10 @@
     for c in range(1, CHUNKS):
         forward.append([exchange(at, c, fwd_out, fwd_in, fwd_sent, fwd_got) for at in range(2)])
     forward = [sum(copies, []) for copies in forward]
-    first_image = send_image(0, first_real[pl.ds(side, 1)].reshape(rows, ny))
+    first_image = send_image(0, 0, 0, first_real[pl.ds(side, 1)].reshape(rows, ny))
 
     turn = (1 - 2 * side).astype(jnp.float32)
+    half = rows // 2
 
     def apply(table, x):
         high, low = split2(x)
@@ -695,6 +697,7 @@
         for one, table in ((upper + lower, even_k), (upper - lower, odd_k)):
             line = apply(table, one)
             spectrum.append((line, jnp.concatenate([line[:, span:], line[:, :span]], 1)))
+        lines = []
         for g in range(REFS):
             sides = []
             for parity, table in enumerate((even_k_t, odd_k_t)):
@@ -703,32 +706,36 @@
                 sides.append(
                     apply(table, line * band_even[c, g, part, :] + swapped * band_odd[c, g, part, :])
                 )
-            back_out[g, c] = (sides[0] + turn * sides[1]).reshape(group, rows, pair)
-            backward.append(exchange(g, c, back_out, back_in, back_sent, back_got))
-    made = []
-    for g in range(REFS):
+            lines.append((sides[0] + turn * sides[1]).reshape(group, rows, pair))
+        both = jnp.concatenate(lines, 2)
+        for h in range(2):
+            back_out[h, c] = both[:, h * half : (h + 1) * half]
+            backward.append(exchange(h, c, back_out, back_in, back_sent, back_got))
+    last_image = []
+    for h in range(2):
         for c in range(CHUNKS):
-            for copy in backward[c * REFS + g]:
+            for copy in backward[2 * c + h]:
                 copy.wait_recv()
-        lines = [
-            jnp.concatenate(
-                [
-                    back_in[g, c, src, :, p * span : (p + 1) * span]
-                    for src in range(group)
-                    for c in range(CHUNKS)
-                ],
-                1,
+        lines = []
+        for at in range(2 * REFS):
+            part = slice(at * span, (at + 1) * span)
+            lines.append(
+                jnp.concatenate(
+                    [back_in[h, c, src, :, part] for src in range(group) for c in range(CHUNKS)], 1
+                )
             )
-            for p in range(2)
+        field = inverse_y(jnp.concatenate(lines, 0))
+        made = [
+            (field[2 * g * half : (2 * g + 1) * half], field[(2 * g + 1) * half : (2 * g + 2) * half])
+            for g in range(REFS)
         ]
-        field = inverse_y(jnp.concatenate(lines, 0))
-        made.append((field[:rows], field[rows:]))
-    real, imag = choose(made, vel_last[...])
-    cosine, sine = along_last[...], across_last[...]
-    moved = real * cosine - imag * sine
-    last_image = send_image(1, moved)
-    wave_ref[0] = moved
-    wave_ref[1] = real * sine + imag * cosine
+        own = slice(h * half, (h + 1) * half)
+        real, imag = choose(made, vel_last[own, :])
+        cosine, sine = along_last[own, :], across_last[own, :]
+        moved = real * cosine - imag * sine
+        last_image += send_image(1 + h, 1, h * half, moved)
+        wave_ref[0, own, :] = moved
+        wave_ref[1, own, :] = real * sine + imag * cosine
 
     leave_route()
     leave_coef()
@@ -818,8 +825,8 @@
             pltpu.VMEM((2, rows, ny), f32),
             pltpu.VMEM((2, CHUNKS, group, rows, pair), f32),
             pltpu.VMEM((2, CHUNKS, group, rows, pair), f32),
-            pltpu.VMEM((REFS, CHUNKS, group, rows, pair), f32),
-            pltpu.VMEM((REFS, CHUNKS, group, rows, pair), f32),
+            pltpu.VMEM((2, CHUNKS, group, rows // 2, REFS * pair), f32),
+            pltpu.VMEM((2, CHUNKS, group, rows // 2, REFS * pair), f32),
             pltpu.VMEM((2, F, rows, ny // F), f32),
             dma((5,)),
             dma((6,)),
@@ -830,10 +837,10 @@
             dma((2 * F,)),
             dma((2, CHUNKS, group)),
             dma((2, CHUNKS, group)),
-            dma((REFS, CHUNKS, group)),
-            dma((REFS, CHUNKS, group)),
-            dma((2, F)),
-            dma((2, F)),
+            dma((2, CHUNKS, group)),
+            dma((2, CHUNKS, group)),
+            dma((3, F)),
+            dma((3, F)),
         ],
         compiler_params=pltpu.CompilerParams(
             collective_id=0, has_side_effects=True, vmem_limit_bytes=40 << 20

time: 44.2 us -> 44.2 us (level)
  no operation moved by 1% of the time
where the time goes in v8:
time: 44.2 us; the launch traced here: 44 us
  Pallas kernels  42.7 us (97%)
  between operations  1.29 us (3%)
    pallas_call x1, Pallas kernels, local(): pl.pallas_call(functools.partial(program, cfg), out_shape=[jax.ShapeDtype...  42 us

profile of v8, /device:TPU:0, one launch (start us, length us, event | category | flops | bytes accessed | tf_op | source)
XLA Modules:
  0.0 44.0 jit_solution(17349446189795042404)
XLA Ops:
  1.3 42.0 %shard_map.122 = (f32[2,64,512]{2,1,0:T(8,128)S(1)}, f32[2,4,64,128]{3,2,1,0:T(8,128)S(1)}) custom-call(f32[2,4,1024]{2,1,0:T(4,128)} %spectra_hbm.1, s32[1,1024]{1,0:T(1,128)} %bitcast.3, s32[1,1024]{1,0:T(1,128)} %bitcast.4, f32[2,1024]{1,0:T(2,128)} %offset_hbm.1, f32[1,1024]{1,0:T(1,128)} %bitcast.5, f32[1]{0:T(128)S(6)} %copy.13.freq_ref, ...), custom_call_target="tpu_custom_call" | custom-call | tf_op jit(solution)/shard_map/pallas_call | solution.py:792
  43.3 0.7 %shard_map.123 = (f32[2,1,64,512]{3,2,1,0:T(8,128)}, f32[2,64,128]{2,1,0:T(8,128)}) custom-call(f32[2,64,512]{2,1,0:T(8,128)S(1)} %get-tuple-element.4.wave_ref, f32[2,4,64,128]{3,2,1,0:T(8,128)S(1)} %get-tuple-element.5.part_ref), custom_call_target="tpu_custom_call" | custom-call | tf_op jit(solution)/shard_map/pallas_call | solution.py:855

commit v9 on v8

--- a/solution.py
+++ b/solution.py
@@ -273,9 +273,12 @@
     parts = jnp.concatenate([high, middle, low], 0)
     fold = (data_rows + 4) // 2
     wide = 256
+    places = iota((wide, count), 0).astype(jnp.float32).astype(jnp.bfloat16)
+    one, none = jnp.ones((), jnp.bfloat16), jnp.zeros((), jnp.bfloat16)
     for at in range(0, devices * slots, wide):
-        places = iota((wide, count), 0) + at
-        chosen = jnp.where(places == slot, 1.0, 0.0).astype(jnp.bfloat16)
+        within = jnp.where((slot >= at) & (slot < at + wide), slot - at, wide)
+        within = within.astype(jnp.float32).astype(jnp.bfloat16)
+        chosen = jnp.where(places == within, one, none)
         got = dot(parts, chosen, NT)
         got = got[:padded] + got[padded : 2 * padded] + got[2 * padded :]
         for piece in range(wide // slots):
@@ -568,7 +571,7 @@
     for which in (1, 3):
         own_high, own_low = hart[which, 0, seat_rows, :], hart[which, 1, seat_rows, :]
         seats.append((own_high, jnp.concatenate([own_high, own_low], 0)))
-    wide = 128
+    wide = 256
     for first in range(0, ny, wide):
         lanes = slice(first, first + wide)
         made = [[None, None] for _ in range(REFS)]

time: 44.2 us -> 43.8 us (level)
    pallas_call x1, Pallas kernels: 42 us -> 41.5 us  [local(): pl.pallas_call(functools.partial(program, cfg), out_shape=[jax.ShapeDtype...]
where the time goes in v9:
time: 43.8 us; the launch traced here: 43.6 us
  Pallas kernels  42.3 us (97%)
  between operations  1.29 us (3%)
    pallas_call x1, Pallas kernels, local(): pl.pallas_call(functools.partial(program, cfg), out_shape=[jax.ShapeDtype...  41.5 us

profile of v9, /device:TPU:0, one launch (start us, length us, event | category | flops | bytes accessed | tf_op | source)
XLA Modules:
  0.0 43.6 jit_solution(13468052491801365056)
XLA Ops:
  1.3 41.5 %shard_map.122 = (f32[2,64,512]{2,1,0:T(8,128)S(1)}, f32[2,4,64,128]{3,2,1,0:T(8,128)S(1)}) custom-call(f32[2,4,1024]{2,1,0:T(4,128)} %spectra_hbm.1, s32[1,1024]{1,0:T(1,128)} %bitcast.3, s32[1,1024]{1,0:T(1,128)} %bitcast.4, f32[2,1024]{1,0:T(2,128)} %offset_hbm.1, f32[1,1024]{1,0:T(1,128)} %bitcast.5, f32[1]{0:T(128)S(6)} %copy.13.freq_ref, ...), custom_call_target="tpu_custom_call" | custom-call | tf_op jit(solution)/shard_map/pallas_call | solution.py:795
  42.8 0.7 %shard_map.123 = (f32[2,1,64,512]{3,2,1,0:T(8,128)}, f32[2,64,128]{2,1,0:T(8,128)}) custom-call(f32[2,64,512]{2,1,0:T(8,128)S(1)} %get-tuple-element.4.wave_ref, f32[2,4,64,128]{3,2,1,0:T(8,128)S(1)} %get-tuple-element.5.part_ref), custom_call_target="tpu_custom_call" | custom-call | tf_op jit(solution)/shard_map/pallas_call | solution.py:858

commit v10 on v9

--- a/solution.py
+++ b/solution.py
@@ -232,10 +232,10 @@
             ]
         )
     ]
+    for load in inputs:
+        load.wait()
     for load in loads:
         load.start()
-    for load in inputs:
-        load.wait()
 
     count = tile_ref.shape[1]
     width = 128

time: 43.8 us -> 43.8 us (level)
  no operation moved by 1% of the time
where the time goes in v10:
time: 43.8 us; the launch traced here: 43.6 us
  Pallas kernels  42.3 us (97%)
  between operations  1.29 us (3%)
    pallas_call x1, Pallas kernels, local(): pl.pallas_call(functools.partial(program, cfg), out_shape=[jax.ShapeDtype...  41.6 us

profile of v10, /device:TPU:0, one launch (start us, length us, event | category | flops | bytes accessed | tf_op | source)
XLA Modules:
  0.0 43.6 jit_solution(10019350861123694849)
XLA Ops:
  1.3 41.6 %shard_map.122 = (f32[2,64,512]{2,1,0:T(8,128)S(1)}, f32[2,4,64,128]{3,2,1,0:T(8,128)S(1)}) custom-call(f32[2,4,1024]{2,1,0:T(4,128)} %spectra_hbm.1, s32[1,1024]{1,0:T(1,128)} %bitcast.3, s32[1,1024]{1,0:T(1,128)} %bitcast.4, f32[2,1024]{1,0:T(2,128)} %offset_hbm.1, f32[1,1024]{1,0:T(1,128)} %bitcast.5, f32[1]{0:T(128)S(6)} %copy.13.freq_ref, ...), custom_call_target="tpu_custom_call" | custom-call | tf_op jit(solution)/shard_map/pallas_call | solution.py:795
  42.8 0.7 %shard_map.123 = (f32[2,1,64,512]{3,2,1,0:T(8,128)}, f32[2,64,128]{2,1,0:T(8,128)}) custom-call(f32[2,64,512]{2,1,0:T(8,128)S(1)} %get-tuple-element.4.wave_ref, f32[2,4,64,128]{3,2,1,0:T(8,128)S(1)} %get-tuple-element.5.part_ref), custom_call_target="tpu_custom_call" | custom-call | tf_op jit(solution)/shard_map/pallas_call | solution.py:858
